TPU v7x, 64 devices: a 2x2x8 block of a 4x4x8 slice. The times are simulated.
64 devices in a mesh: batch: 4 (over x, y), seq: 16 (over z, core).
Axes of the slice: x: 2, y: 2, z: 8, core: 2. Of those that a mesh axis runs over, the one named last changes fastest.
The devices are a block of a 4x4x8 slice.
Arguments:
- msa_act: bfloat16 [512, 256, 256], P(('batch', 'seq')), parts along dimension 0
- msa_mask: int32 [512, 256], P(('batch', 'seq')), parts along dimension 0
- pair_act: bfloat16 [1024, 256, 128], P(('batch', 'seq')), parts along dimension 0
- w_pair_bias: bfloat16 [128, 8], replicated
- w_row_in: bfloat16 [256, 1024], replicated
- w_row_out: bfloat16 [256, 256], replicated
- w_col_in: bfloat16 [256, 576], replicated
- w_col_out: bfloat16 [256, 256], replicated
- w_trans_in: bfloat16 [256, 1024], replicated
- w_trans_out: bfloat16 [1024, 256], replicated
Outputs:
- output: bfloat16 [512, 256, 256], P('batch', 'seq'), parts along dimension 0
There are 4 independent parts. A program takes and returns all parts, laid end to end along the dimension named above; an argument that names none is the same for every part.
All inputs are finite; a program needn't handle non-finite values.
Results may differ from a plain program's by a relative error of at most 0.0144833.
Values are sent between devices in bfloat16 or wider.
A program may use at most 768 MiB of HBM per device.

v0:
```python
import jax
import jax.numpy as jnp
from jax import lax
from jax.sharding import PartitionSpec as P

LN_EPS = 1.0e-5
MASK_BIG = 1.0e9
MEAN_EPS = 1.0e-10


def layer_norm(x_in):
    x_f32 = x_in.astype(jnp.float32)
    mean_val = jnp.mean(x_f32, axis=-1, keepdims=True)
    centered = x_f32 - mean_val
    var_val = jnp.mean(centered * centered, axis=-1, keepdims=True)
    return (centered * lax.rsqrt(var_val + LN_EPS)).astype(jnp.bfloat16)


def pick_tile(n_rows, per_row):
    budget = 2 ** 22
    best_tile = 1
    for candidate in range(1, n_rows + 1):
        if n_rows % candidate == 0 and candidate * per_row <= budget:
            best_tile = candidate
    return best_tile


def row_attention(value_a7, mask_bias, bias_hij, w_row_in, w_row_out):
    n_seq, n_res, n_chans = value_a7.shape
    n_heads = bias_hij.shape[0]
    head_dim = w_row_out.shape[0] // n_heads
    qk_scale = head_dim ** -0.5
    w_row_split = w_row_in.reshape(n_chans, 4, n_heads, head_dim)
    row_proj = jnp.einsum('snc,cfhd->fsnhd', layer_norm(value_a7), w_row_split, preferred_element_type=jnp.float32).astype(jnp.bfloat16)
    tile_rows = pick_tile(n_seq, n_heads * n_res * n_res)
    n_tiles = n_seq // tile_rows
    tiled_proj = row_proj.reshape(4, n_tiles, tile_rows, n_res, n_heads, head_dim)

    def tile_body(packed):
        q_tile, k_tile, v_tile, m_tile = packed
        logits = jnp.einsum('sihd,sjhd->shij', q_tile, k_tile, preferred_element_type=jnp.float32) * qk_scale
        logits = logits + bias_hij[None] + m_tile[:, None, None, :]
        attn_probs = jax.nn.softmax(logits, axis=-1).astype(jnp.bfloat16)
        return jnp.einsum('shij,sjhd->sihd', attn_probs, v_tile, preferred_element_type=jnp.float32)

    attended = lax.map(tile_body, (tiled_proj[0], tiled_proj[1], tiled_proj[2], mask_bias.reshape(n_tiles, tile_rows, n_res)))
    attended = attended.reshape(n_seq, n_res, n_heads, head_dim)
    gated_row = (jax.nn.sigmoid(row_proj[3].astype(jnp.float32)) * attended).astype(jnp.bfloat16)
    row_update = jnp.einsum('snhd,hdc->snc', gated_row, w_row_out.reshape(n_heads, head_dim, n_chans), preferred_element_type=jnp.float32)
    return (value_a7.astype(jnp.float32) + row_update).astype(jnp.bfloat16)


def column_attention(value_a7, value_a8, w_col_in, w_col_out, n_heads):
    n_seq, n_res, n_chans = value_a7.shape
    head_ch = w_col_out.shape[0]
    head_dim = head_ch // n_heads
    col_proj = jnp.einsum('snc,cf->snf', layer_norm(value_a7), w_col_in, preferred_element_type=jnp.float32).astype(jnp.bfloat16)
    queries = col_proj[:, :, :head_ch].reshape(n_seq, n_res, n_heads, head_dim)
    col_keys = col_proj[:, :, head_ch:head_ch + head_dim]
    col_vals = col_proj[:, :, head_ch + head_dim:head_ch + 2 * head_dim]
    col_gates = col_proj[:, :, head_ch + 2 * head_dim:].reshape(n_seq, n_res, n_heads, head_dim)
    mask_f32 = value_a8.astype(jnp.float32)
    q_sum = jnp.einsum('sn,snhd->nhd', value_a8.astype(jnp.bfloat16), queries, preferred_element_type=jnp.float32)
    mask_count = jnp.sum(mask_f32, axis=0)
    q_sum, mask_count = lax.psum((q_sum, mask_count), 'seq')
    q_mean = (q_sum / (mask_count + MEAN_EPS)[:, None, None]).astype(jnp.bfloat16)
    col_logits = jnp.einsum('nhd,snd->snh', q_mean, col_keys, preferred_element_type=jnp.float32) * head_dim ** -0.5
    col_logits = col_logits + (MASK_BIG * (mask_f32 - 1.0))[:, :, None]
    loc_max = jnp.max(col_logits, axis=0)
    weights = jnp.exp(col_logits - loc_max[None])
    loc_den = jnp.sum(weights, axis=0)
    loc_num = jnp.einsum('snh,snd->nhd', weights, col_vals, preferred_element_type=jnp.float32)
    glob_max = lax.pmax(loc_max, 'seq')
    rescale = jnp.exp(loc_max - glob_max)
    glob_den, glob_num = lax.psum((loc_den * rescale, loc_num * rescale[:, :, None]), 'seq')
    col_out = glob_num / glob_den[:, :, None]
    gated_col = (jax.nn.sigmoid(col_gates.astype(jnp.float32)) * col_out[None]).astype(jnp.bfloat16)
    col_update = jnp.einsum('snhd,hdc->snc', gated_col, w_col_out.reshape(n_heads, head_dim, n_chans), preferred_element_type=jnp.float32)
    return (value_a7.astype(jnp.float32) + col_update).astype(jnp.bfloat16)


def transition(value_a7, w_trans_in, w_trans_out):
    hidden = jnp.einsum('snc,cf->snf', layer_norm(value_a7), w_trans_in, preferred_element_type=jnp.float32)
    hidden = jnp.maximum(hidden, 0.0).astype(jnp.bfloat16)
    trans_update = jnp.einsum('snf,fc->snc', hidden, w_trans_out, preferred_element_type=jnp.float32)
    return (value_a7.astype(jnp.float32) + trans_update).astype(jnp.bfloat16)


def solution(mesh):
    def local_block(value_a7, value_a8, pair_act, w_pair_bias, w_row_in, w_row_out, w_col_in, w_col_out, w_trans_in, w_trans_out):
        n_heads = w_pair_bias.shape[1]
        bias_rows = jnp.einsum('ijc,ch->hij', layer_norm(pair_act), w_pair_bias, preferred_element_type=jnp.float32).astype(jnp.bfloat16)
        bias_full = lax.all_gather(bias_rows, 'seq', axis=1, tiled=True)
        mask_bias = MASK_BIG * (value_a8.astype(jnp.float32) - 1.0)
        after_row = row_attention(value_a7, mask_bias, bias_full, w_row_in, w_row_out)
        after_col = column_attention(after_row, value_a8, w_col_in, w_col_out, n_heads)
        after_trans = transition(after_col, w_trans_in, w_trans_out)
        return lax.all_to_all(after_trans, 'seq', 1, 0, tiled=True)

    rows_spec = P(('batch', 'seq'))
    return jax.shard_map(local_block, mesh=mesh, in_specs=(rows_spec, rows_spec, rows_spec, P(), P(), P(), P(), P(), P(), P()), out_specs=P('batch', 'seq'), check_vma=False)
```

profile of v0, /device:TPU:21, one launch (start us, length us, event | category | flops | bytes accessed | tf_op | source)
XLA Modules:
  0.0 399.9 jit_solution(7180380860348438735)
XLA Ops:
  6.6 1.7 convert_reduce_fusion.3
  8.4 2.3 fusion.26
  10.8 2.1 fusion.34
  14.6 29.2 %psum.29 = f32[256]{0:T(256)S(1)} all-reduce(f32[256]{0:T(256)S(1)} %get-tuple-element.28), channel_id=1, replica_groups=mesh['batch'=4,'seq'=16] {'seq'}, use_global_device_ids=true, to_apply=%region_10.11 | all-reduce | flops 256 | bytes 2048 | tf_op jit(solution)/shard_map/psum | solution.py:65
  44.3 3.2 convert_bitcast_fusion
  47.5 5.9 %all-gather.2.cloned.1.call-done = bf16[8,256,256]{2,0,1:T(8,128)(2,1)} async-done(((bf16[8,16,256]{2,0,1:T(8,128)(2,1)}), bf16[8,256,256]{2,0,1:T(8,128)(2,1)}) %all-gather.2.cloned.1.call-update) | async-done | bytes 1048592 | tf_op jit(solution)/shard_map/all_gather | solution.py:93
  53.4 2.9 copy.51
  56.2 11.4 %fusion.68 = (f32[8,8,256]{2,1,0:T(8,128)S(1)}, f32[8,8,256,256]{2,3,1,0:T(8,128)}) fusion(f32[8,256]{1,0:T(8,128)S(1)} %get-tuple-element.30, f32[8,256,256]{1,2,0:T(8,128)} %copy.51, bf16[4,8,256,8,32]{2,4,3,0,1:T(8,128)(2,1)} %convert_bitcast_fusion), kind=kOutput, calls=%fused_computation.101 | convolution fusion | flops 289407232 | bytes 21045248 | tf_op jit(solution)/shard_map/while/body/eval_jaxpr/sub | solution.py:43
  67.7 8.5 %convert_reduce_fusion.1 = (f32[8,256]{1,0:T(8,128)S(1)}, bf16[8,256,256]{1,2,0:T(8,128)(2,1)S(1)}) fusion(bf16[8,32,256,1]{2,1,0,3:T(8,128)(2,1)S(1)} %bitcast.97, f32[8,8,256,256]{2,3,1,0:T(8,128)} %get-tuple-element.33, f32[8,8,256]{2,1,0:T(8,128)S(1)} %get-tuple-element.32, bf16[4,8,256,8,32]{2,4,3,0,1:T(8,128)(2,1)} %convert_bitcast_fusion, ...), kind=kOutput, calls=%fused_computation.19 | convolution fusion | flops 551024640 | bytes 21176320 | tf_op jit(solution)/shard_map/snhd,hdc->snc/dot_general | solution.py:49
  77.2 2.0 convolution_convert_fusion
  82.6 102.2 %all-reduce.3.cloned.1.call-done = f32[256,8,32]{2,1,0:T(8,128)} async-done(((f32[256,8,32]{2,1,0:T(8,128)}), f32[256,8,32]{2,1,0:T(8,128)}) %all-reduce.3.cloned.1.call-update) | async-done | bytes 262160 | tf_op jit(solution)/shard_map/psum | solution.py:65
  184.8 3.1 fusion.69
  187.9 47.1 %pmax.7 = f32[256,8]{1,0:T(8,128)} all-reduce(f32[256,8]{1,0:T(8,128)S(1)} %get-tuple-element.36), channel_id=1, replica_groups=mesh['batch'=4,'seq'=16] {'seq'}, use_global_device_ids=true, to_apply=%region_12.13 | all-reduce | flops 2048 | bytes 16384 | tf_op jit(solution)/shard_map/pmax | solution.py:73
  235.0 1.7 fusion.54
  236.8 1.6 fusion.66
  238.3 1.6 convolution_multiply_fusion
  240.0 1.9 add_divide_fusion
  241.9 46.6 %psum.31 = f32[256,8]{1,0:T(8,128)S(1)} all-reduce(f32[256,8]{1,0:T(8,128)S(1)} %copy-done.6), channel_id=1, replica_groups=mesh['batch'=4,'seq'=16] {'seq'}, use_global_device_ids=true, to_apply=%region_15.16 | all-reduce | flops 2048 | bytes 16384 | tf_op jit(solution)/shard_map/psum | solution.py:75
  288.5 58.7 %all-reduce.5.cloned.1.call-done = f32[256,8,32]{2,1,0:T(8,128)} async-done(((f32[256,8,32]{2,1,0:T(8,128)}), f32[256,8,32]{2,1,0:T(8,128)}) %all-reduce.5.cloned.1.call-update) | async-done | bytes 262160 | tf_op jit(solution)/shard_map/psum | solution.py:75
  347.2 1.6 broadcast_divide_fusion
  349.1 2.2 convert_reduce_fusion
  351.7 4.4 %fusion.30 = bf16[8,256,256]{1,2,0:T(8,128)(2,1)} fusion(bf16[8,256,256]{1,2,0:T(8,128)(2,1)S(1)} %get-tuple-element.39, f32[8,256]{1,0:T(8,128)S(1)} %add_rsqrt_fusion.1, f32[8,256]{1,0:T(8,128)S(1)} %broadcast_multiply_fusion.1, bf16[1024,256]{1,0:T(8,128)(2,1)S(1)} %copy-done, bf16[256,1024]{1,0:T(8,128)(2,1)} %param.18), kind=kOutput, calls=%fused_computation.44 | convolution fusion | flops 2155347968 | bytes 3162112 | tf_op jit(solution)/shard_map/snf,fc->snc/dot_general | solution.py:85
  356.1 1.9 copy.61
  357.9 34.2 %all_to_all.18 = bf16[8,256,256]{2,0,1:T(8,128)(2,1)S(1)} all-to-all(bf16[8,256,256]{2,0,1:T(8,128)(2,1)S(1)} %copy.61), channel_id=1, replica_groups=mesh['batch'=4,'seq'=16] {'seq'}, dimensions={1} | all-to-all | bytes 2097152 | tf_op jit(solution)/shard_map/all_to_all | solution.py:98
  (58 shorter events, 8.5 us)
Async XLA Ops:
  6.5 345.1 %copy-start = (bf16[1024,256]{1,0:T(8,128)(2,1)S(1)}, bf16[1024,256]{1,0:T(8,128)(2,1)}, u32[]{:S(2)}) copy-start(bf16[1024,256]{1,0:T(8,128)(2,1)} %param.19) | copy-start | bytes 1572868
  6.6 4.2 %copy-start.3 = (bf16[16,256,128]{2,1,0:T(8,128)(2,1)S(1)}, bf16[16,256,128]{2,1,0:T(8,128)(2,1)}, u32[]{:S(2)}) copy-start(bf16[16,256,128]{2,1,0:T(8,128)(2,1)} %param.12) | copy-start | bytes 3145732
  6.6 4.2 %copy-start.12 = (bf16[128,8]{0,1:T(8,128)(2,1)S(1)}, bf16[128,8]{0,1:T(8,128)(2,1)}, u32[]{:S(2)}) copy-start(bf16[128,8]{0,1:T(8,128)(2,1)} %param.13) | copy-start | bytes 6148
  6.6 6.4 %copy-start.5 = (bf16[8,256,256]{2,1,0:T(8,128)(2,1)S(1)}, bf16[8,256,256]{2,1,0:T(8,128)(2,1)}, u32[]{:S(2)}) copy-start(bf16[8,256,256]{2,1,0:T(8,128)(2,1)} %param.10) | copy-start | bytes 3145732
  6.6 46.8 %all-gather.2.cloned.1.call-start = ((), (), s32[]{:S(2)}) async-start(), calls=%async_computation.1 | async-start | bytes 1114112 | tf_op jit(solution)/shard_map/all_gather | solution.py:93
  10.7 2.8 copy-start.7
  10.8 3.0 copy-start.10
  12.9 171.9 %all-reduce.3.cloned.1.call-start = ((), (), s32[]{:S(2)}) async-start(), calls=%async_computation.2 | async-start | bytes 2097152 | tf_op jit(solution)/shard_map/psum | solution.py:65
  56.2 11.4 %copy-start.11 = (bf16[256,256]{1,0:T(8,128)(2,1)S(1)}, bf16[256,256]{1,0:T(8,128)(2,1)}, u32[]{:S(2)}) copy-start(bf16[256,256]{1,0:T(8,128)(2,1)} %param.15) | copy-start | bytes 393220
  67.7 9.5 %copy-start.8 = (bf16[256,576]{0,1:T(8,128)(2,1)S(1)}, bf16[256,576]{0,1:T(8,128)(2,1)}, u32[]{:S(2)}) copy-start(bf16[256,576]{0,1:T(8,128)(2,1)} %param.16) | copy-start | bytes 884740
  76.2 1.0 copy-start.1
  80.9 266.3 %all-reduce.5.cloned.1.call-start = ((), (), s32[]{:S(2)}) async-start(), calls=%async_computation.3 | async-start | bytes 2097152 | tf_op jit(solution)/shard_map/psum | solution.py:75
  235.0 3.3 copy-start.4
  239.9 2.0 copy-start.6
  241.9 107.2 %copy-start.2 = (bf16[8,256,256]{1,2,0:T(8,128)(2,1)S(1)}, bf16[8,256,256]{1,2,0:T(8,128)(2,1)}, u32[]{:S(2)}) copy-start(bf16[8,256,256]{1,2,0:T(8,128)(2,1)} %copy-done.1) | copy-start | bytes 3145732
  241.9 107.2 %copy-start.9 = (bf16[256,256]{1,0:T(8,128)(2,1)S(1)}, bf16[256,256]{1,0:T(8,128)(2,1)}, u32[]{:S(2)}) copy-start(bf16[256,256]{1,0:T(8,128)(2,1)} %param.17) | copy-start | bytes 393220
Sparse Core Ops, SparseCore 0:
  13.0 40.2 all-gather.1
  81.1 103.7 all-reduce.2
  240.1 107.0 all-reduce.4
where the time goes:
time: 400 us
  waiting for transfers between devices  167 us (42%)
  blocking collectives  157 us (39%)
  matrix products  38.5 us (10%)
  between operations  13.4 us (3%)
  other arithmetic  12.1 us (3%)
  local copies, waits for them, and re-layouts  11.4 us (3%)
    psum x1, waiting for transfers between devices, column_attention(): q_sum, mask_count = lax.psum((q_sum, mask_count), 'seq')  102 us
    psum x1, waiting for transfers between devices, column_attention(): lax.psum((loc_den * rescale, loc_num * rescale[:, :, None]), 'seq')  58.7 us
    pmax x1, blocking collectives, column_attention(): glob_max = lax.pmax(loc_max, 'seq')  47.1 us
    psum x1, blocking collectives, column_attention(): lax.psum((loc_den * rescale, loc_num * rescale[:, :, None]), 'seq')  46.6 us
    all_to_all x1, blocking collectives, local_block(): return lax.all_to_all(after_trans, 'seq', 1, 0, tiled=True)  34.2 us
    psum x1, blocking collectives, column_attention(): q_sum, mask_count = lax.psum((q_sum, mask_count), 'seq')  29.2 us
    sub x1, matrix products, tile_body(): attn_probs = jax.nn.softmax(logits, axis=-1).astype(jnp.bfloat16)  11.4 us
    dot_general x1, matrix products, row_attention(): jnp.einsum('snhd,hdc->snc', gated_row, w_row_out.reshape(n_heads, head_di...  8.53 us
  transfers between devices with their start and end apart: 3, of which 3 were waited for; matrix products, arithmetic and copies ran while one was open for 2% of the time, Pallas kernels for 0%

commit v1 on v0

--- a/solution.py
+++ b/solution.py
@@ -62,18 +62,11 @@
     mask_f32 = value_a8.astype(jnp.float32)
     q_sum = jnp.einsum('sn,snhd->nhd', value_a8.astype(jnp.bfloat16), queries, preferred_element_type=jnp.float32)
     mask_count = jnp.sum(mask_f32, axis=0)
-    q_sum, mask_count = lax.psum((q_sum, mask_count), 'seq')
     q_mean = (q_sum / (mask_count + MEAN_EPS)[:, None, None]).astype(jnp.bfloat16)
     col_logits = jnp.einsum('nhd,snd->snh', q_mean, col_keys, preferred_element_type=jnp.float32) * head_dim ** -0.5
     col_logits = col_logits + (MASK_BIG * (mask_f32 - 1.0))[:, :, None]
-    loc_max = jnp.max(col_logits, axis=0)
-    weights = jnp.exp(col_logits - loc_max[None])
-    loc_den = jnp.sum(weights, axis=0)
-    loc_num = jnp.einsum('snh,snd->nhd', weights, col_vals, preferred_element_type=jnp.float32)
-    glob_max = lax.pmax(loc_max, 'seq')
-    rescale = jnp.exp(loc_max - glob_max)
-    glob_den, glob_num = lax.psum((loc_den * rescale, loc_num * rescale[:, :, None]), 'seq')
-    col_out = glob_num / glob_den[:, :, None]
+    probs = jax.nn.softmax(col_logits, axis=0)
+    col_out = jnp.einsum('snh,snd->nhd', probs, col_vals, preferred_element_type=jnp.float32)
     gated_col = (jax.nn.sigmoid(col_gates.astype(jnp.float32)) * col_out[None]).astype(jnp.bfloat16)
     col_update = jnp.einsum('snhd,hdc->snc', gated_col, w_col_out.reshape(n_heads, head_dim, n_chans), preferred_element_type=jnp.float32)
     return (value_a7.astype(jnp.float32) + col_update).astype(jnp.bfloat16)
@@ -93,9 +86,10 @@
         bias_full = lax.all_gather(bias_rows, 'seq', axis=1, tiled=True)
         mask_bias = MASK_BIG * (value_a8.astype(jnp.float32) - 1.0)
         after_row = row_attention(value_a7, mask_bias, bias_full, w_row_in, w_row_out)
-        after_col = column_attention(after_row, value_a8, w_col_in, w_col_out, n_heads)
-        after_trans = transition(after_col, w_trans_in, w_trans_out)
-        return lax.all_to_all(after_trans, 'seq', 1, 0, tiled=True)
+        after_row = lax.all_to_all(after_row, 'seq', 1, 0, tiled=True)
+        mask_cols = lax.all_to_all(value_a8, 'seq', 1, 0, tiled=True)
+        after_col = column_attention(after_row, mask_cols, w_col_in, w_col_out, n_heads)
+        return transition(after_col, w_trans_in, w_trans_out)
 
     rows_spec = P(('batch', 'seq'))
     return jax.shard_map(local_block, mesh=mesh, in_specs=(rows_spec, rows_spec, rows_spec, P(), P(), P(), P(), P(), P(), P()), out_specs=P('batch', 'seq'), check_vma=False)

time: 400 us -> 133 us (0.33)
  blocking collectives: 157 us -> 0 us
  waiting for transfers between devices: 167 us -> 49.9 us
  starting transfers between devices: 0.37 us -> 15.4 us
  matrix products: 38.5 us -> 34.1 us
    psum x2 -> x0, waiting for transfers between devices: 161 us -> none  [the longest x1 102 us: column_attention(): q_sum, mask_count = lax.psum((q_sum, mask_count), 'seq')]
    psum x2 -> x0, blocking collectives: 75.8 us -> none  [the longest x1 46.6 us: column_attention(): lax.psum((loc_den * rescale, loc_num * rescale[:, :, None]), 'seq')]
    pmax x1 -> x0, blocking collectives: 47.1 us -> none  [column_attention(): glob_max = lax.pmax(loc_max, 'seq')]
    all_to_all x1 -> x0, blocking collectives: 34.2 us -> none  [local_block(): return lax.all_to_all(after_trans, 'seq', 1, 0, tiled=True)]
    all_to_all x0 -> x2, waiting for transfers between devices: none -> 25.2 us  [the longest x1 25.2 us: local_block(): after_row = lax.all_to_all(after_row, 'seq', 1, 0, tiled=True)]
    all_gather x1, waiting for transfers between devices: 5.87 us -> 24.6 us  [local_block(): bias_full = lax.all_gather(bias_rows, 'seq', axis=1, tiled=True)]
    all_to_all x0 -> x2, starting transfers between devices: none -> 15.4 us  [the longest x1 10.7 us: local_block(): mask_cols = lax.all_to_all(value_a8, 'seq', 1, 0, tiled=True)]
  transfers between devices with their start and end apart: 3 -> 3, of which waited for: 3 -> 2; matrix products, arithmetic and copies ran while one was open for 2% -> 23% of each run, Pallas kernels for 0% -> 0%
where the time goes in v1:
time: 133 us
  waiting for transfers between devices  49.9 us (38%)
  matrix products  34.1 us (26%)
  starting transfers between devices  15.4 us (12%)
  between operations  13.8 us (10%)
  other arithmetic  10.5 us (8%)
  local copies, waits for them, and re-layouts  8.99 us (7%)
    all_to_all x1, waiting for transfers between devices, local_block(): after_row = lax.all_to_all(after_row, 'seq', 1, 0, tiled=True)  25.2 us
    all_gather x1, waiting for transfers between devices, local_block(): bias_full = lax.all_gather(bias_rows, 'seq', axis=1, tiled=True)  24.6 us
    sub x1, matrix products, tile_body(): attn_probs = jax.nn.softmax(logits, axis=-1).astype(jnp.bfloat16)  11.4 us
    all_to_all x1, starting transfers between devices, local_block(): mask_cols = lax.all_to_all(value_a8, 'seq', 1, 0, tiled=True)  10.7 us
    dot_general x1, matrix products, row_attention(): jnp.einsum('snhd,hdc->snc', gated_row, w_row_out.reshape(n_heads, head_di...  8.41 us
    reduce_sum x4, other arithmetic, layer_norm(): var_val = jnp.mean(centered * centered, axis=-1, keepdims=True)  4.74 us
    all_to_all x1, starting transfers between devices, local_block(): after_row = lax.all_to_all(after_row, 'seq', 1, 0, tiled=True)  4.63 us
    dot_general x1, matrix products, transition(): jnp.einsum('snf,fc->snc', hidden, w_trans_out, preferred_element_type=jnp...  4.18 us
  transfers between devices with their start and end apart: 3, of which 2 were waited for; matrix products, arithmetic and copies ran while one was open for 23% of the time, Pallas kernels for 0%

profile of v1, /device:TPU:21, one launch (start us, length us, event | category | flops | bytes accessed | tf_op | source)
XLA Modules:
  0.0 132.7 jit_solution(4543558583466053163)
XLA Ops:
  6.6 1.7 %convert_reduce_fusion.2 = f32[16,256]{1,0:T(8,128)S(1)} fusion(bf16[16,256,128]{2,1,0:T(8,128)(2,1)} %param.12), kind=kLoop, calls=%fused_computation.22 | loop fusion | flops 1044480 | bytes 1064960 | tf_op jit(solution)/shard_map/reduce_sum | solution.py:13
  8.4 2.4 %fusion.22 = f32[16,256]{1,0:T(8,128)S(1)} fusion(bf16[16,256,128]{2,1,0:T(8,128)(2,1)} %param.12, f32[16,256]{1,0:T(8,128)S(1)} %broadcast_multiply_fusion.1), kind=kLoop, calls=%fused_computation.33 | loop fusion | flops 2093056 | bytes 1081344 | tf_op jit(solution)/shard_map/reduce_sum | solution.py:15
  10.8 2.1 %fusion.32 = bf16[8,16,256]{2,0,1:T(8,128)(2,1)} fusion(bf16[16,256,128]{2,1,0:T(8,128)(2,1)S(1)} %copy-done.2, f32[16,256]{1,0:T(8,128)S(1)} %add_rsqrt_fusion.1, f32[16,256]{1,0:T(8,128)S(1)} %broadcast_multiply_fusion.1, bf16[128,8]{0,1:T(8,128)(2,1)S(1)} %copy-done.10), kind=kOutput, calls=%fused_computation.52 | convolution fusion | flops 10518528 | bytes 1148928 | tf_op jit(solution)/shard_map/ijc,ch->hij/dot_general | solution.py:85
  13.1 0.7 reshape.160
  13.8 10.7 %all-to-all-start.1 = ((s32[16,1,128]{2,1,0:T(1,128)}), s32[16,1,128]{2,1,0:T(1,128)S(1)}, u32[]{:S(2)}, u32[]{:S(2)}) async-start(s32[16,1,128]{2,1,0:T(1,128)} %reshape.160), calls=%async_computation.1 | async-start | bytes 16384 | tf_op jit(solution)/shard_map/all_to_all | solution.py:90
  25.1 0.6 fusion.20
  25.8 3.1 %convert_bitcast_fusion = bf16[4,8,256,8,32]{2,4,3,0,1:T(8,128)(2,1)} fusion(bf16[256,4,8,32,1]{0,3,2,1,4:T(8,128)(2,1)S(1)} %bitcast.127, bf16[8,256,256]{2,1,0:T(8,128)(2,1)S(1)} %copy-done.1, f32[8,256]{1,0:T(8,128)S(1)} %add_rsqrt_fusion.3, f32[8,256]{1,0:T(8,128)S(1)} %broadcast_multiply_fusion.3), kind=kOutput, calls=%fused_computation.12 | convolution fusion | flops 1077936128 | bytes 5783552 | tf_op jit(solution)/shard_map/snc,cfhd->fsnhd/dot_general | solution.py:34
  28.9 24.6 %all-gather.2.cloned.1.call-done = bf16[8,256,256]{2,0,1:T(8,128)(2,1)} async-done(((bf16[8,16,256]{2,0,1:T(8,128)(2,1)}), bf16[8,256,256]{2,0,1:T(8,128)(2,1)}) %all-gather.2.cloned.1.call-update) | async-done | bytes 1048592 | tf_op jit(solution)/shard_map/all_gather | solution.py:86
  53.5 2.9 %copy.28 = f32[8,256,256]{1,2,0:T(8,128)} copy(bf16[8,256,256]{2,0,1:T(8,128)(2,1)} %all-gather.2.cloned.1.call-done) | data formatting | bytes 3145728 | tf_op jit(solution)/shard_map/while/body/eval_jaxpr/convert_element_type | solution.py:42
  56.4 11.4 %fusion.71 = (f32[8,8,256]{2,1,0:T(8,128)S(1)}, f32[8,8,256,256]{2,3,1,0:T(8,128)}) fusion(f32[8,256]{1,0:T(8,128)S(1)} %add_multiply_fusion, f32[8,256,256]{1,2,0:T(8,128)} %copy.28, bf16[4,8,256,8,32]{2,4,3,0,1:T(8,128)(2,1)} %convert_bitcast_fusion), kind=kOutput, calls=%fused_computation.106 | convolution fusion | flops 289407232 | bytes 21045248 | tf_op jit(solution)/shard_map/while/body/eval_jaxpr/sub | solution.py:43
  67.8 8.4 %fusion.24 = bf16[8,256,256]{2,1,0:T(8,128)(2,1)S(1)} fusion(bf16[8,256,256]{2,1,0:T(8,128)(2,1)S(1)} %copy-done.1, bf16[8,32,256,1]{2,1,0,3:T(8,128)(2,1)S(1)} %bitcast.133, f32[8,8,256,256]{2,3,1,0:T(8,128)} %get-tuple-element.30, f32[8,8,256]{2,1,0:T(8,128)S(1)} %get-tuple-element.28, bf16[4,8,256,8,32]{2,4,3,0,1:T(8,128)(2,1)} %convert_bitcast_fusion), kind=kOutput, calls=%fused_computation.35 | convolution fusion | flops 549978112 | bytes 21168128 | tf_op jit(solution)/shard_map/snhd,hdc->snc/dot_general | solution.py:49
  76.2 1.6 %copy.30 = bf16[8,256,256]{2,0,1:T(8,128)(2,1)} copy(bf16[8,256,256]{2,1,0:T(8,128)(2,1)S(1)} %fusion.24) | data formatting | bytes 2097152 | tf_op jit(solution)/shard_map/convert_element_type | solution.py:50
  77.8 4.6 %all-to-all-start = ((bf16[8,256,256]{2,0,1:T(8,128)(2,1)}), bf16[8,256,256]{2,0,1:T(8,128)(2,1)}, u32[]{:S(2)}, u32[]{:S(2)}) async-start(bf16[8,256,256]{2,0,1:T(8,128)(2,1)} %copy.30), calls=%async_computation | async-start | bytes 2097152 | tf_op jit(solution)/shard_map/all_to_all | solution.py:89
  83.0 0.7 reduce.4
  84.0 25.2 %all-to-all-done = bf16[8,256,256]{2,0,1:T(8,128)(2,1)} async-done(((bf16[8,256,256]{2,0,1:T(8,128)(2,1)}), bf16[8,256,256]{2,0,1:T(8,128)(2,1)}, u32[]{:S(2)}, u32[]{:S(2)}) %all-to-all-start) | async-done | bytes 1048608 | tf_op jit(solution)/shard_map/all_to_all | solution.py:89
  109.2 1.5 %bitcast_convert_fusion = (f32[8,16,16,256]{3,0,2,1:T(8,128)S(1)}, f32[16,8,16,256]{3,1,2,0:T(8,128)S(1)}) fusion(bf16[8,256,256]{2,0,1:T(8,128)(2,1)} %all-to-all-done), kind=kLoop, calls=%fused_computation.75 | loop fusion | flops 524288 | bytes 5242880 | tf_op jit(solution)/shard_map/convert_element_type | solution.py:72
  110.7 0.6 bitcast_reduce_fusion
  111.4 1.0 fusion.30
  112.7 1.3 %convolution_convert_fusion = bf16[128,16,576]{0,2,1:T(8,128)(2,1)S(1)} fusion(f32[16,8,16,256]{3,1,2,0:T(8,128)S(1)} %get-tuple-element.18, f32[128,16]{0,1:T(8,128)S(1)} %copy.36, f32[128,16]{0,1:T(8,128)S(1)} %copy.34, bf16[256,576]{0,1:T(8,128)(2,1)S(1)} %copy-done.5), kind=kOutput, calls=%fused_computation.50 | convolution fusion | flops 606732288 | bytes 4767744 | tf_op jit(solution)/shard_map/snc,cf->snf/dot_general | solution.py:57
  114.7 1.4 %fusion.73 = f32[16,1,8,32]{3,1,2,0:T(1,128)S(1)} fusion(bf16[128,16,8,32]{0,3,2,1:T(8,128)(2,1)S(1)} %bitcast.126, bf16[128,16,1,1]{0,2,3,1:T(2,128)(2,1)S(1)} %copy.43), kind=kOutput, calls=%fused_computation.109 | convolution fusion | flops 1048576 | bytes 1069056 | tf_op jit(solution)/shard_map/sn,snhd->nhd/dot_general | solution.py:63
  116.9 1.6 %convert_reduce_fusion = (f32[128,16]{0,1:T(8,128)S(1)}, bf16[128,16,256]{2,0,1:T(8,128)(2,1)S(1)}) fusion(bf16[8,32,256,1]{2,1,0,3:T(8,128)(2,1)S(1)} %bitcast.131, f32[128,16,8,32]{0,3,2,1:T(8,128)S(1)} %bitcast.125, f32[16,8,32]{2,1,0:T(8,128)S(1)} %fusion.59, f32[16,8,16,256]{3,1,2,0:T(8,128)S(1)} %get-tuple-element.18), kind=kOutput, calls=%fused_computation.16 | convolution fusion | flops 271579136 | bytes 5398528 | tf_op jit(solution)/shard_map/snhd,hdc->snc/dot_general | solution.py:71
  118.5 0.9 copy-done.3
  120.1 4.2 %fusion.25 = bf16[128,16,256]{2,0,1:T(8,128)(2,1)S(1)} fusion(bf16[128,16,256]{2,0,1:T(8,128)(2,1)} %copy-done.3, f32[128,16]{0,1:T(8,128)S(1)} %add_rsqrt_fusion.2, f32[128,16]{0,1:T(8,128)S(1)} %broadcast_multiply_fusion.2, bf16[1024,256]{1,0:T(8,128)(2,1)S(1)} %copy-done, bf16[256,1024]{1,0:T(8,128)(2,1)S(1)} %copy-done.8), kind=kOutput, calls=%fused_computation.36 | convolution fusion | flops 2155347968 | bytes 3162112 | tf_op jit(solution)/shard_map/snf,fc->snc/dot_general | solution.py:78
  124.3 1.6 %copy.39 = bf16[128,16,256]{2,1,0:T(8,128)(2,1)} copy(bf16[128,16,256]{2,0,1:T(8,128)(2,1)S(1)} %fusion.25) | data formatting | bytes 2097152 | tf_op jit(solution)/shard_map/convert_element_type | solution.py:79
  (54 shorter events, 3.9 us)
Async XLA Ops:
  6.5 113.5 %copy-start = (bf16[1024,256]{1,0:T(8,128)(2,1)S(1)}, bf16[1024,256]{1,0:T(8,128)(2,1)}, u32[]{:S(2)}) copy-start(bf16[1024,256]{1,0:T(8,128)(2,1)} %param.19) | copy-start | bytes 1572868
  6.6 4.3 %copy-start.2 = (bf16[16,256,128]{2,1,0:T(8,128)(2,1)S(1)}, bf16[16,256,128]{2,1,0:T(8,128)(2,1)}, u32[]{:S(2)}) copy-start(bf16[16,256,128]{2,1,0:T(8,128)(2,1)} %param.12) | copy-start | bytes 3145732
  6.6 4.3 %copy-start.10 = (bf16[128,8]{0,1:T(8,128)(2,1)S(1)}, bf16[128,8]{0,1:T(8,128)(2,1)}, u32[]{:S(2)}) copy-start(bf16[128,8]{0,1:T(8,128)(2,1)} %param.13) | copy-start | bytes 6148
  6.6 6.4 %copy-start.7 = (s32[8,256]{1,0:T(8,128)S(1)}, s32[8,256]{1,0:T(8,128)}, u32[]{:S(2)}) copy-start(s32[8,256]{1,0:T(8,128)} %param.11) | copy-start | bytes 24580
  6.6 18.0 %copy-start.4 = (bf16[256,1024]{1,0:T(8,128)(2,1)S(1)}, bf16[256,1024]{1,0:T(8,128)(2,1)}, u32[]{:S(2)}) copy-start(bf16[256,1024]{1,0:T(8,128)(2,1)} %param.14) | copy-start | bytes 1572868
  6.6 46.9 %all-gather.2.cloned.1.call-start = ((), (), s32[]{:S(2)}) async-start(), calls=%async_computation.2 | async-start | bytes 1114112 | tf_op jit(solution)/shard_map/all_gather | solution.py:86
  8.4 16.4 %copy-start.1 = (bf16[8,256,256]{2,1,0:T(8,128)(2,1)S(1)}, bf16[8,256,256]{2,1,0:T(8,128)(2,1)}, u32[]{:S(2)}) copy-start(bf16[8,256,256]{2,1,0:T(8,128)(2,1)} %param.10) | copy-start | bytes 3145732
  13.8 64.0 %all-to-all-start.1 = ((s32[16,1,128]{2,1,0:T(1,128)}), s32[16,1,128]{2,1,0:T(1,128)S(1)}, u32[]{:S(2)}, u32[]{:S(2)}) async-start(s32[16,1,128]{2,1,0:T(1,128)} %reshape.160), calls=%async_computation.1 | async-start | bytes 16384 | tf_op jit(solution)/shard_map/all_to_all | solution.py:90
  56.4 11.4 %copy-start.9 = (bf16[256,256]{1,0:T(8,128)(2,1)S(1)}, bf16[256,256]{1,0:T(8,128)(2,1)}, u32[]{:S(2)}) copy-start(bf16[256,256]{1,0:T(8,128)(2,1)} %param.15) | copy-start | bytes 393220
  77.8 31.4 %all-to-all-start = ((bf16[8,256,256]{2,0,1:T(8,128)(2,1)}), bf16[8,256,256]{2,0,1:T(8,128)(2,1)}, u32[]{:S(2)}, u32[]{:S(2)}) async-start(bf16[8,256,256]{2,0,1:T(8,128)(2,1)} %copy.30), calls=%async_computation | async-start | bytes 2097152 | tf_op jit(solution)/shard_map/all_to_all | solution.py:89
  110.7 1.9 %copy-start.5 = (bf16[256,576]{0,1:T(8,128)(2,1)S(1)}, bf16[256,576]{0,1:T(8,128)(2,1)}, u32[]{:S(2)}) copy-start(bf16[256,576]{0,1:T(8,128)(2,1)} %param.16) | copy-start | bytes 884740
  114.1 2.7 %copy-start.6 = (bf16[256,256]{1,0:T(8,128)(2,1)S(1)}, bf16[256,256]{1,0:T(8,128)(2,1)}, u32[]{:S(2)}) copy-start(bf16[256,256]{1,0:T(8,128)(2,1)} %param.17) | copy-start | bytes 393220
  116.8 3.2 %copy-start.8 = (bf16[256,1024]{1,0:T(8,128)(2,1)S(1)}, bf16[256,1024]{1,0:T(8,128)(2,1)}, u32[]{:S(2)}) copy-start(bf16[256,1024]{1,0:T(8,128)(2,1)} %param.18) | copy-start | bytes 1572868
  118.4 1.0 copy-start.3
Sparse Core Ops, SparseCore 0:
  13.1 40.3 all-gather.1

commit v2 on v1

v2 whole, which is shorter than its diff:
```python
import functools

import jax
import jax.numpy as jnp
from jax import lax
from jax.experimental import pallas as pl
from jax.experimental.pallas import tpu as pltpu
from jax.sharding import PartitionSpec as P

MESH = pl.DeviceIdType.MESH
LN_EPS = 1.0e-5
MASK_BIG = 1.0e9
MEAN_EPS = 1.0e-10
LOG2E = 1.4426950408889634
EXCLUDED = -3.0e38
F32 = jnp.float32
BF16 = jnp.bfloat16
NT = (((1,), (1,)), ((), ()))


def layer_norm(x_in):
    x = x_in.astype(F32)
    centered = x - jnp.mean(x, axis=-1, keepdims=True)
    var = jnp.mean(centered * centered, axis=-1, keepdims=True)
    return (centered * lax.rsqrt(var + LN_EPS)).astype(BF16)


def dot(a, b):
    return jnp.dot(a, b, preferred_element_type=F32)


def dot_nt(a, b):
    return lax.dot_general(a, b, NT, preferred_element_type=F32)


def iota(shape, dim):
    return lax.broadcasted_iota(jnp.int32, shape, dim)


def block_kernel(dims, e_hbm, m_hbm, z_hbm, wpb_hbm, wri_hbm, wro_hbm, wci_hbm, wco_hbm, wti_hbm, wto_hbm, out_hbm,
                 e_v, m_v, z_v, wpb_v, wri_v, wro_v, wci_v, wco_v, wti_v, wto_v,
                 bias32, bias_all, q_s, k_s, v_s, g_s, mb_s, hm_s, bias_t, gt_s, e1_send, e1_recv,
                 wc_s, mrow_s, qsum_s, kt_s, vt_s, gc_s, x_s, p3_s, co_s, out_v,
                 in_sem, out_sem, chain_sem, pair_sem, bias_sem, send_sem, recv_sem):
    n_dev, n_seq, n_res, ch, heads = dims
    chips = n_dev // 2
    reach = chips // 2
    blk = n_res // n_dev
    hd = ch // heads
    c2 = hd ** -0.5 * LOG2E
    hrows = heads * blk
    prows = n_seq * blk
    me = lax.axis_index("seq")
    z, c = lax.div(me, 2), lax.rem(me, 2)

    def chip_at(offset):
        return lax.rem(z + offset + chips, chips)

    def slot_of(chip, core):
        return chip * 2 + core

    loads = [(z_hbm, z_v), (wpb_hbm, wpb_v), (e_hbm, e_v), (m_hbm, m_v), (wri_hbm, wri_v), (wro_hbm, wro_v),
             (wci_hbm, wci_v), (wco_hbm, wco_v), (wti_hbm, wti_v), (wto_hbm, wto_v)]
    copies = [pltpu.make_async_copy(src, dst, in_sem.at[n]) for n, (src, dst) in enumerate(loads)]
    for copy in copies:
        copy.start()

    barrier = pltpu.get_barrier_semaphore()
    for d in range(1, n_dev):
        pl.semaphore_signal(barrier, inc=1, device_id={"seq": lax.rem(me + d, n_dev)}, device_id_type=MESH)

    copies[0].wait()
    copies[1].wait()
    wpb_t = wpb_v[...]

    def bias_row(i, carry):
        rows = dot_nt(wpb_t, layer_norm(z_v[i]))
        for n in range(n_res // 128):
            bias32[n, pl.ds(i, heads, stride=blk), :] = rows[:, n * 128:(n + 1) * 128]
        return carry

    lax.fori_loop(0, blk, bias_row, 0, unroll=True)
    bias_all[me, :hrows] = jnp.concatenate([bias32[n] for n in range(n_res // 128)], axis=-1).astype(BF16)
    copies[3].wait()
    m_f32 = m_v[...].astype(F32)
    mb_s[...] = (MASK_BIG * LOG2E) * (m_f32 - 1.0)
    bias_all[me, hrows:] = jnp.concatenate([m_f32, m_f32], axis=0).astype(BF16)
    pl.semaphore_wait(barrier, n_dev - 1)

    def bias_copy(slot, sem, chip, core):
        return pltpu.make_async_remote_copy(
            src_ref=bias_all.at[slot], dst_ref=bias_all.at[slot], send_sem=sem, recv_sem=bias_sem.at[slot],
            device_id={"seq": slot_of(chip, core)}, device_id_type=MESH)

    def up(k):
        return bias_copy(slot_of(chip_at(-k), c), chain_sem.at[0, k], chip_at(1), c)

    def down(k):
        return bias_copy(slot_of(chip_at(k), c), chain_sem.at[1, k], chip_at(-1), c)

    def across(offset, t):
        return bias_copy(slot_of(chip_at(offset), c), pair_sem.at[t], z, 1 - c)

    def bias_wait(offset, core):
        bias_copy(slot_of(chip_at(offset), core), pair_sem.at[0], z, c).wait_recv()

    up(0).start()
    down(0).start()
    across(0, 0).start()

    for h in range(heads):
        hm_s[h] = jnp.where(lax.div(iota((blk, ch), 1), hd) == h, 1.0, 0.0).astype(BF16)
    copies[2].wait()
    copies[4].wait()

    def project(s, carry):
        proj = dot(layer_norm(e_v[s]), wri_v[...]).astype(BF16)
        q_s[s] = proj[:, :ch]
        k_s[s] = proj[:, ch:2 * ch]
        v_s[s] = proj[:, 2 * ch:3 * ch]
        g_s[s] = proj[:, 3 * ch:]
        return carry

    lax.fori_loop(0, n_seq, project, 0)
    copies[5].wait()

    lane_head = lax.div(iota((blk, ch), 1), hd)

    def own_head(blocks):
        picked = blocks[0]
        for h in range(1, heads):
            picked = jnp.where(lane_head == h, blocks[h], picked)
        return picked

    def e1_copy(t, core):
        chip = tile_chip(t)
        return pltpu.make_async_remote_copy(
            src_ref=e1_send.at[t, core], dst_ref=e1_recv.at[me], send_sem=send_sem.at[t, core], recv_sem=recv_sem.at[me],
            device_id={"seq": slot_of(chip, core)}, device_id_type=MESH)

    def tile_offset(t):
        k = lax.div(t + 1, 2)
        return k * (1 - 2 * lax.rem(t, 2))

    def tile_chip(t):
        return chip_at(tile_offset(t))

    def row_tile(t, carry):
        k = lax.div(t + 1, 2)

        @pl.when(lax.rem(t, 2) == 1)
        def _():
            bias_wait(-k, c)
            across(-k, t).start()

            @pl.when(k < reach)
            def _():
                up(k).start()
                bias_wait(k, c)
                across(k, t + 1).start()

            @pl.when(k < reach - 1)
            def _():
                down(k).start()

        bias_wait(tile_offset(t), 1 - c)
        chip = tile_chip(t)
        for core in range(2):
            bias_t[core * hrows:(core + 1) * hrows] = bias_all[slot_of(chip, core), :hrows].astype(F32) * LOG2E
        first = pl.multiple_of(chip * (2 * blk), 2 * blk)

        def sequence(s, carry):
            parts = []
            for core in range(2):
                q_rows = q_s[s, pl.ds(first + core * blk, blk), :]
                parts += [q_rows * hm_s[h] for h in range(heads)]
            logits = dot_nt(jnp.concatenate(parts, axis=0), k_s[s])
            mask_row = mb_s[pl.ds(s, 1), :]
            probs = []
            step = hrows // 2
            for r in range(0, 2 * hrows, step):
                x = logits[r:r + step] * c2 + (bias_t[r:r + step] + mask_row)
                p = jnp.exp2(x - jnp.max(x, axis=-1, keepdims=True))
                probs.append((p * (1.0 / jnp.sum(p, axis=-1, keepdims=True))).astype(BF16))
            attended = dot(jnp.concatenate(probs, axis=0), v_s[s])
            for core in range(2):
                o = own_head([attended[core * hrows + h * blk:core * hrows + (h + 1) * blk] for h in range(heads)])
                gate = jax.nn.sigmoid(g_s[s, pl.ds(first + core * blk, blk), :].astype(F32))
                gt_s[core, s] = (gate * o).astype(BF16)
            return carry

        lax.fori_loop(0, n_seq, sequence, 0)
        update = dot(gt_s[...].reshape(2 * prows, ch), wro_v[...])
        for core in range(2):
            e_rows = e_v[:, pl.ds(first + core * blk, blk), :].reshape(prows, ch).astype(F32)
            e1_send[t, core] = (e_rows + update[core * prows:(core + 1) * prows]).astype(BF16)

        @pl.when(t == 0)
        def _():
            e1_recv[me] = e1_send[0, c]
            e1_copy(0, 1 - c).start()

        @pl.when(t > 0)
        def _():
            e1_copy(t, 0).start()
            e1_copy(t, 1).start()

        return carry

    lax.fori_loop(0, chips, row_tile, 0)

    copies[6].wait()
    w_k, w_v = wci_v[ch:ch + hd], wci_v[ch + hd:ch + 2 * hd]
    w_all = jnp.concatenate([wci_v[:ch]] + [w_k] * heads + [w_v] * heads + [wci_v[ch + 2 * hd:]], axis=0)
    eye = jnp.where(iota((ch, ch), 0) == iota((ch, ch), 1), 1.0, 0.0).astype(BF16)
    wc_s[...] = dot_nt(eye, w_all).astype(BF16)

    pad = 2 * n_seq
    m_all = bias_all[:, hrows:, :].reshape(n_dev * pad, n_res)
    pick = jnp.where(iota((n_res, prows), 0) == me * blk + lax.rem(iota((n_res, prows), 1), blk), 1.0, 0.0).astype(BF16)
    m_sel = dot(m_all, pick)
    m_sel = jnp.where(lax.rem(iota((n_dev * pad, prows), 0), pad) == lax.div(iota((n_dev * pad, prows), 1), blk), m_sel, 0.0)
    mrow_s[...] = jnp.sum(m_sel.reshape(n_dev, pad, prows), axis=1)
    same = lax.rem(iota((blk, 2 * prows), 1), blk) == iota((blk, 2 * prows), 0)
    qsum_s[...] = jnp.zeros_like(qsum_s)

    def pair_mask(chip):
        return jnp.concatenate([mrow_s[pl.ds(chip * 2 + core, 1), :] for core in range(2)], axis=1)

    def column_in(t, carry):
        chip = chip_at(-tile_offset(t))

        def arrival(core):
            slot = slot_of(chip, core)
            pltpu.make_async_remote_copy(
                src_ref=e1_send.at[0, 0], dst_ref=e1_recv.at[slot], send_sem=send_sem.at[0, 0], recv_sem=recv_sem.at[slot],
                device_id={"seq": me}, device_id_type=MESH).wait_recv()

        @pl.when(t == 0)
        def _():
            arrival(1 - c)

        @pl.when(t > 0)
        def _():
            arrival(0)
            arrival(1)

        rows = e1_recv[pl.ds(chip * 2, 2)].reshape(2 * prows, ch)
        proj = dot(layer_norm(rows), wc_s[...]).astype(BF16)
        kt_s[chip] = proj[:, ch:2 * ch]
        vt_s[chip] = proj[:, 2 * ch:3 * ch]
        gc_s[chip] = proj[:, 3 * ch:]
        sel = jnp.where(same, pair_mask(chip), 0.0).astype(BF16)
        qsum_s[...] += dot(sel, proj[:, :ch])
        return carry

    lax.fori_loop(0, chips, column_in, 0)

    same1 = same[:, :prows]
    count = jnp.sum(jnp.where(same1, jnp.sum(mrow_s[...], axis=0, keepdims=True), 0.0), axis=-1, keepdims=True)
    q_mean = (qsum_s[...] / (count + MEAN_EPS)).astype(BF16)
    q_rows = jnp.concatenate([q_mean * hm_s[h] for h in range(heads)], axis=0)
    same_h = lax.rem(iota((hrows, 2 * prows), 1), blk) == lax.rem(iota((hrows, 2 * prows), 0), blk)
    top = jnp.full((hrows, 2 * prows), EXCLUDED, F32)
    for chip in range(chips):
        x = dot_nt(q_rows, kt_s[chip]) * c2 + (MASK_BIG * LOG2E) * (pair_mask(chip) - 1.0)
        x = jnp.where(same_h, x, EXCLUDED)
        x_s[chip] = x
        top = jnp.maximum(top, x)
    top = jnp.max(top, axis=-1, keepdims=True)
    total = jnp.zeros((hrows, 2 * prows), F32)
    for chip in range(chips):
        p = jnp.exp2(x_s[chip] - top)
        total = total + p
        for n in range(3):
            piece = p.astype(BF16)
            p3_s[n * hrows:(n + 1) * hrows, chip * 2 * prows:(chip + 1) * 2 * prows] = piece
            p = p - piece.astype(F32)
    o3 = dot(p3_s[...], vt_s[...].reshape(chips * 2 * prows, ch))
    o = (o3[:hrows] + o3[hrows:2 * hrows] + o3[2 * hrows:]) / jnp.sum(total, axis=-1, keepdims=True)
    co_s[...] = own_head([o[h * blk:(h + 1) * blk] for h in range(heads)])

    copies[7].wait()
    copies[8].wait()
    copies[9].wait()

    def finish(chip, carry):
        e1 = e1_recv[pl.ds(chip * 2, 2)].reshape(2 * prows, ch).astype(F32)
        gate = jax.nn.sigmoid(gc_s[chip].astype(F32)).reshape(2 * n_seq, blk, ch)
        gated = (gate * co_s[...][None]).astype(BF16).reshape(2 * prows, ch)
        e2 = (e1 + dot(gated, wco_v[...])).astype(BF16)
        hidden = jnp.maximum(dot(layer_norm(e2), wti_v[...]), 0.0).astype(BF16)
        e3 = (e2.astype(F32) + dot(hidden, wto_v[...])).astype(BF16)
        out_v[pl.ds(chip * 2 * n_seq, 2 * n_seq)] = e3.reshape(2 * n_seq, blk, ch)
        out_copy(chip).start()
        return carry

    def out_copy(chip):
        rows = pl.ds(chip * 2 * n_seq, 2 * n_seq)
        return pltpu.make_async_copy(out_v.at[rows], out_hbm.at[rows], out_sem.at[chip])

    lax.fori_loop(0, chips, finish, 0)

    for k in range(reach):
        up(k).wait_send()
        if k < reach - 1:
            down(k).wait_send()
    for t in range(chips):
        across(0, t).wait_send()
    e1_copy(0, 1 - c).wait_send()
    for t in range(1, chips):
        e1_copy(t, 0).wait_send()
        e1_copy(t, 1).wait_send()
    for chip in range(chips):
        out_copy(chip).wait()


def solution(mesh):
    n_dev = mesh.shape["seq"]

    def local_block(e, m, z, w_pair_bias, w_row_in, w_row_out, w_col_in, w_col_out, w_trans_in, w_trans_out):
        n_seq, n_res, ch = e.shape
        heads = w_pair_bias.shape[1]
        blk = n_res // n_dev
        chips = n_dev // 2
        hrows, prows = heads * blk, n_seq * blk
        args = (e, m, z, w_pair_bias.T, w_row_in, w_row_out, w_col_in.T, w_col_out, w_trans_in, w_trans_out)
        scratch = [pltpu.VMEM(a.shape, a.dtype) for a in args] + [
            pltpu.VMEM((n_res // 128, hrows, 128), F32),
            pltpu.VMEM((n_dev, hrows + 2 * n_seq, n_res), BF16),
            pltpu.VMEM((n_seq, n_res, ch), BF16),
            pltpu.VMEM((n_seq, n_res, ch), BF16),
            pltpu.VMEM((n_seq, n_res, ch), BF16),
            pltpu.VMEM((n_seq, n_res, ch), BF16),
            pltpu.VMEM((n_seq, n_res), F32),
            pltpu.VMEM((heads, blk, ch), BF16),
            pltpu.VMEM((2 * hrows, n_res), F32),
            pltpu.VMEM((2, n_seq, blk, ch), BF16),
            pltpu.VMEM((chips, 2, prows, ch), BF16),
            pltpu.VMEM((n_dev, prows, ch), BF16),
            pltpu.VMEM((ch, 4 * ch), BF16),
            pltpu.VMEM((n_dev, prows), F32),
            pltpu.VMEM((blk, ch), F32),
            pltpu.VMEM((chips, 2 * prows, ch), BF16),
            pltpu.VMEM((chips, 2 * prows, ch), BF16),
            pltpu.VMEM((chips, 2 * prows, ch), BF16),
            pltpu.VMEM((chips, hrows, 2 * prows), F32),
            pltpu.VMEM((3 * hrows, n_dev * prows), BF16),
            pltpu.VMEM((blk, ch), F32),
            pltpu.VMEM((n_dev * n_seq, blk, ch), BF16),
            pltpu.SemaphoreType.DMA((len(args),)),
            pltpu.SemaphoreType.DMA((chips,)),
            pltpu.SemaphoreType.DMA((2, chips // 2)),
            pltpu.SemaphoreType.DMA((chips,)),
            pltpu.SemaphoreType.DMA((n_dev,)),
            pltpu.SemaphoreType.DMA((chips, 2)),
            pltpu.SemaphoreType.DMA((n_dev,)),
        ]
        return pl.pallas_call(
            functools.partial(block_kernel, (n_dev, n_seq, n_res, ch, heads)),
            out_shape=jax.ShapeDtypeStruct((n_dev * n_seq, blk, ch), BF16),
            in_specs=[pl.BlockSpec(memory_space=pl.ANY)] * len(args),
            out_specs=pl.BlockSpec(memory_space=pl.ANY),
            scratch_shapes=scratch,
            name="msa_block",
            compiler_params=pltpu.CompilerParams(collective_id=0, has_side_effects=True, vmem_limit_bytes=60 * 2 ** 20),
        )(*args)

    rows_spec = P(('batch', 'seq'))
    return jax.shard_map(local_block, mesh=mesh, in_specs=(rows_spec, rows_spec, rows_spec, P(), P(), P(), P(), P(), P(), P()), out_specs=P('batch', 'seq'), check_vma=False)
```

time: 133 us -> 80 us (0.60)
  Pallas kernels: 0 us -> 77.6 us
  waiting for transfers between devices: 49.9 us -> 0 us
  matrix products: 34.1 us -> 0 us
  starting transfers between devices: 15.4 us -> 0 us
  between operations: 13.8 us -> 0.01 us
  other arithmetic: 10.5 us -> 0 us
  local copies, waits for them, and re-layouts: 8.99 us -> 2.26 us
    pallas_call x0 -> x1, Pallas kernels: none -> 77.6 us  [local_block(): pl.pallas_call(functools.partial(block_kernel, (n_dev, n_seq, n_res, ch,...]
    all_to_all x2 -> x0, waiting for transfers between devices: 25.2 us -> none  [the longest x1 25.2 us: local_block(): after_row = lax.all_to_all(after_row, 'seq', 1, 0, tiled=True)]
    all_gather x1 -> x0, waiting for transfers between devices: 24.6 us -> none  [local_block(): bias_full = lax.all_gather(bias_rows, 'seq', axis=1, tiled=True)]
    dot_general x9 -> x0, matrix products: 22.7 us -> none  [the longest x1 8.41 us: row_attention(): jnp.einsum('snhd,hdc->snc', gated_row, w_row_out.reshape(n_heads, head_di...]
    all_to_all x2 -> x0, starting transfers between devices: 15.4 us -> none  [the longest x1 10.7 us: local_block(): mask_cols = lax.all_to_all(value_a8, 'seq', 1, 0, tiled=True)]
    sub x1 -> x0, matrix products: 11.4 us -> none  [tile_body(): attn_probs = jax.nn.softmax(logits, axis=-1).astype(jnp.bfloat16)]
    reduce_sum x9 -> x0, other arithmetic: 7.66 us -> none  [the longest x4 4.74 us: layer_norm(): var_val = jnp.mean(centered * centered, axis=-1, keepdims=True)]
    convert_element_type x4 -> x0, local copies, waits for them, and re-layouts: 6.05 us -> none  [the longest x1 2.88 us: tile_body(): logits = logits + bias_hij[None] + m_tile[:, None, None, :]]
  transfers between devices with their start and end apart: 3 -> 0, of which waited for: 2 -> 0; matrix products, arithmetic and copies ran while one was open for 23% -> 0% of each run, Pallas kernels for 0% -> 0%
where the time goes in v2:
time: 80 us; the launch traced here: 79.9 us
  Pallas kernels  77.6 us (97%)
  local copies, waits for them, and re-layouts  2.26 us (3%)
    pallas_call x1, Pallas kernels, local_block(): pl.pallas_call(functools.partial(block_kernel, (n_dev, n_seq, n_res, ch,...  77.6 us
    unnamed x1, local copies, waits for them, and re-layouts  2.26 us

profile of v2, /device:TPU:21, one launch (start us, length us, event | category | flops | bytes accessed | tf_op | source)
XLA Modules:
  0.0 79.9 jit_solution(3922420276986745734)
XLA Ops:
  0.0 77.6 %msa_block.1 = bf16[128,16,256]{2,1,0:T(8,128)(2,1)} custom-call(bf16[8,256,256]{2,1,0:T(8,128)(2,1)} %e_hbm.1, s32[8,256]{1,0:T(8,128)} %m_hbm.1, bf16[16,256,128]{2,1,0:T(8,128)(2,1)} %z_hbm.1, bf16[8,128]{1,0:T(8,128)(2,1)} %bitcast.3, bf16[256,1024]{1,0:T(8,128)(2,1)} %wri_hbm.1, bf16[256,256]{1,0:T(8,128)(2,1)} %wro_hbm.1, bf16[576,256]{1,0:T(8,128)(2,1)} %bitcast.2, ...), custom_call_target="tpu_custom_call" | custom-call | tf_op jit(solution)/shard_map/msa_block/pallas_call | solution.py:359
  77.6 2.3 %copy.12 = bf16[128,16,256]{2,1,0:T(8,128)(2,1)} copy(bf16[128,16,256]{2,1,0:T(8,128)(2,1)} %msa_block.1) | data formatting | bytes 2097152

commit v3 on v2

--- a/solution.py
+++ b/solution.py
@@ -121,7 +121,7 @@
         g_s[s] = proj[:, 3 * ch:]
         return carry
 
-    lax.fori_loop(0, n_seq, project, 0)
+    lax.fori_loop(0, n_seq, project, 0, unroll=True)
     copies[5].wait()
 
     lane_head = lax.div(iota((blk, ch), 1), hd)
@@ -169,13 +169,17 @@
             bias_t[core * hrows:(core + 1) * hrows] = bias_all[slot_of(chip, core), :hrows].astype(F32) * LOG2E
         first = pl.multiple_of(chip * (2 * blk), 2 * blk)
 
-        def sequence(s, carry):
+        def logits_of(s):
             parts = []
             for core in range(2):
                 q_rows = q_s[s, pl.ds(first + core * blk, blk), :]
                 parts += [q_rows * hm_s[h] for h in range(heads)]
-            logits = dot_nt(jnp.concatenate(parts, axis=0), k_s[s])
-            mask_row = mb_s[pl.ds(s, 1), :]
+            return dot_nt(jnp.concatenate(parts, axis=0), k_s[s])
+
+        logits = logits_of(0)
+        for s in range(n_seq):
+            ahead = logits_of(s + 1) if s + 1 < n_seq else None
+            mask_row = mb_s[s:s + 1, :]
             probs = []
             step = hrows // 2
             for r in range(0, 2 * hrows, step):
@@ -187,9 +191,7 @@
                 o = own_head([attended[core * hrows + h * blk:core * hrows + (h + 1) * blk] for h in range(heads)])
                 gate = jax.nn.sigmoid(g_s[s, pl.ds(first + core * blk, blk), :].astype(F32))
                 gt_s[core, s] = (gate * o).astype(BF16)
-            return carry
-
-        lax.fori_loop(0, n_seq, sequence, 0)
+            logits = ahead
         update = dot(gt_s[...].reshape(2 * prows, ch), wro_v[...])
         for core in range(2):
             e_rows = e_v[:, pl.ds(first + core * blk, blk), :].reshape(prows, ch).astype(F32)
@@ -284,7 +286,12 @@
     copies[8].wait()
     copies[9].wait()
 
-    def finish(chip, carry):
+    def finish(pair, carry):
+        for n in range(2):
+            finish_chip(pair * 2 + n)
+        return carry
+
+    def finish_chip(chip):
         e1 = e1_recv[pl.ds(chip * 2, 2)].reshape(2 * prows, ch).astype(F32)
         gate = jax.nn.sigmoid(gc_s[chip].astype(F32)).reshape(2 * n_seq, blk, ch)
         gated = (gate * co_s[...][None]).astype(BF16).reshape(2 * prows, ch)
@@ -293,13 +300,12 @@
         e3 = (e2.astype(F32) + dot(hidden, wto_v[...])).astype(BF16)
         out_v[pl.ds(chip * 2 * n_seq, 2 * n_seq)] = e3.reshape(2 * n_seq, blk, ch)
         out_copy(chip).start()
-        return carry
 
     def out_copy(chip):
         rows = pl.ds(chip * 2 * n_seq, 2 * n_seq)
         return pltpu.make_async_copy(out_v.at[rows], out_hbm.at[rows], out_sem.at[chip])
 
-    lax.fori_loop(0, chips, finish, 0)
+    lax.fori_loop(0, chips // 2, finish, 0)
 
     for k in range(reach):
         up(k).wait_send()

time: 80 us -> 57.1 us (0.71)
  Pallas kernels: 77.6 us -> 54.7 us
    pallas_call x1, Pallas kernels: 77.6 us -> 54.7 us  [local_block(): pl.pallas_call(functools.partial(block_kernel, (n_dev, n_seq, n_res, ch,...]
where the time goes in v3:
time: 57.1 us; the launch traced here: 57 us
  Pallas kernels  54.7 us (96%)
  local copies, waits for them, and re-layouts  2.26 us (4%)
    pallas_call x1, Pallas kernels, local_block(): pl.pallas_call(functools.partial(block_kernel, (n_dev, n_seq, n_res, ch,...  54.7 us
    unnamed x1, local copies, waits for them, and re-layouts  2.26 us

profile of v3, /device:TPU:21, one launch (start us, length us, event | category | flops | bytes accessed | tf_op | source)
XLA Modules:
  0.0 57.0 jit_solution(7274827735573434900)
XLA Ops:
  0.0 54.7 %msa_block.1 = bf16[128,16,256]{2,1,0:T(8,128)(2,1)} custom-call(bf16[8,256,256]{2,1,0:T(8,128)(2,1)} %e_hbm.1, s32[8,256]{1,0:T(8,128)} %m_hbm.1, bf16[16,256,128]{2,1,0:T(8,128)(2,1)} %z_hbm.1, bf16[8,128]{1,0:T(8,128)(2,1)} %bitcast.3, bf16[256,1024]{1,0:T(8,128)(2,1)} %wri_hbm.1, bf16[256,256]{1,0:T(8,128)(2,1)} %wro_hbm.1, bf16[576,256]{1,0:T(8,128)(2,1)} %bitcast.2, ...), custom_call_target="tpu_custom_call" | custom-call | tf_op jit(solution)/shard_map/msa_block/pallas_call | solution.py:365
  54.7 2.3 %copy.12 = bf16[128,16,256]{2,1,0:T(8,128)(2,1)} copy(bf16[128,16,256]{2,1,0:T(8,128)(2,1)} %msa_block.1) | data formatting | bytes 2097152

commit v4 on v3

--- a/solution.py
+++ b/solution.py
@@ -40,8 +40,8 @@
 def block_kernel(dims, e_hbm, m_hbm, z_hbm, wpb_hbm, wri_hbm, wro_hbm, wci_hbm, wco_hbm, wti_hbm, wto_hbm, out_hbm,
                  e_v, m_v, z_v, wpb_v, wri_v, wro_v, wci_v, wco_v, wti_v, wto_v,
                  bias32, bias_all, q_s, k_s, v_s, g_s, mb_s, hm_s, bias_t, gt_s, e1_send, e1_recv,
-                 wc_s, mrow_s, qsum_s, kt_s, vt_s, gc_s, x_s, p3_s, co_s, out_v,
-                 in_sem, out_sem, chain_sem, pair_sem, bias_sem, send_sem, recv_sem):
+                 relay_v, wc_s, mrow_s, qsum_s, kt_s, vt_s, gc_s, x_s, p3_s, co_s, out_v,
+                 in_sem, out_sem, chain_sem, pair_sem, bias_sem, send_sem, recv_sem, relay_sem, hand_sem):
     n_dev, n_seq, n_res, ch, heads = dims
     chips = n_dev // 2
     reach = chips // 2
@@ -49,7 +49,8 @@
     hd = ch // heads
     c2 = hd ** -0.5 * LOG2E
     hrows = heads * blk
-    prows = n_seq * blk
+    half = blk // 2
+    prows = n_seq * half
     me = lax.axis_index("seq")
     z, c = lax.div(me, 2), lax.rem(me, 2)
 
@@ -132,11 +133,27 @@
             picked = jnp.where(lane_head == h, blocks[h], picked)
         return picked
 
-    def e1_copy(t, core):
-        chip = tile_chip(t)
+    def e1_copy(t, core, hf):
         return pltpu.make_async_remote_copy(
-            src_ref=e1_send.at[t, core], dst_ref=e1_recv.at[me], send_sem=send_sem.at[t, core], recv_sem=recv_sem.at[me],
-            device_id={"seq": slot_of(chip, core)}, device_id_type=MESH)
+            src_ref=e1_send.at[t, hf, core], dst_ref=e1_recv.at[hf, me], send_sem=send_sem.at[t, hf, core],
+            recv_sem=recv_sem.at[hf, me], device_id={"seq": slot_of(tile_chip(t), core)}, device_id_type=MESH)
+
+    def hand_over(core, hf):
+        return pltpu.make_async_remote_copy(
+            src_ref=e1_send.at[chips - 1, hf, core], dst_ref=relay_v.at[core, hf], send_sem=send_sem.at[chips - 1, hf, core],
+            recv_sem=relay_sem.at[core, hf], device_id={"seq": slot_of(chip_at(1 - 2 * core), c)}, device_id_type=MESH)
+
+    def hand_on(core, hf):
+        way = 1 - 2 * core
+        source = slot_of(chip_at(-way), c)
+        return pltpu.make_async_remote_copy(
+            src_ref=relay_v.at[core, hf], dst_ref=e1_recv.at[hf, source], send_sem=hand_sem.at[core, hf],
+            recv_sem=recv_sem.at[hf, source], device_id={"seq": slot_of(chip_at(way * (reach - 1)), core)}, device_id_type=MESH)
+
+    def relay(hf):
+        for core in range(2):
+            hand_over(core, hf).wait_recv()
+            hand_on(core, hf).start()
 
     def tile_offset(t):
         k = lax.div(t + 1, 2)
@@ -190,26 +207,42 @@
             for core in range(2):
                 o = own_head([attended[core * hrows + h * blk:core * hrows + (h + 1) * blk] for h in range(heads)])
                 gate = jax.nn.sigmoid(g_s[s, pl.ds(first + core * blk, blk), :].astype(F32))
-                gt_s[core, s] = (gate * o).astype(BF16)
+                gated = gate * o
+                for hf in range(2):
+                    gt_s[hf, core, s] = gated[hf * half:(hf + 1) * half]
             logits = ahead
-        update = dot(gt_s[...].reshape(2 * prows, ch), wro_v[...])
+        update = dot(gt_s[...].reshape(4 * prows, ch).astype(BF16), wro_v[...])
         for core in range(2):
-            e_rows = e_v[:, pl.ds(first + core * blk, blk), :].reshape(prows, ch).astype(F32)
-            e1_send[t, core] = (e_rows + update[core * prows:(core + 1) * prows]).astype(BF16)
+            e_rows = e_v[:, pl.ds(first + core * blk, blk), :].astype(F32)
+            for hf in range(2):
+                r = (hf * 2 + core) * prows
+                e_half = e_rows[:, hf * half:(hf + 1) * half, :].reshape(prows, ch)
+                e1_send[t, hf, core] = (e_half + update[r:r + prows]).astype(BF16)
 
         @pl.when(t == 0)
         def _():
-            e1_recv[me] = e1_send[0, c]
-            e1_copy(0, 1 - c).start()
-
-        @pl.when(t > 0)
+            for hf in range(2):
+                e1_recv[hf, me] = e1_send[0, hf, c]
+                e1_copy(0, 1 - c, hf).start()
+
+        @pl.when(jnp.logical_and(t > 0, t < chips - 1))
         def _():
-            e1_copy(t, 0).start()
-            e1_copy(t, 1).start()
+            e1_copy(t, 0, 0).start()
+            e1_copy(t, 1, 0).start()
 
         return carry
 
     lax.fori_loop(0, chips, row_tile, 0)
+    for hf in range(2):
+        for core in range(2):
+            hand_over(core, hf).start()
+
+    def second_halves(first_t, last_t):
+        for t in range(first_t, last_t):
+            for core in range(2):
+                e1_copy(t, core, 1).start()
+
+    second_halves(1, 3)
 
     copies[6].wait()
     w_k, w_v = wci_v[ch:ch + hd], wci_v[ch + hd:ch + 2 * hd]
@@ -219,93 +252,119 @@
 
     pad = 2 * n_seq
     m_all = bias_all[:, hrows:, :].reshape(n_dev * pad, n_res)
-    pick = jnp.where(iota((n_res, prows), 0) == me * blk + lax.rem(iota((n_res, prows), 1), blk), 1.0, 0.0).astype(BF16)
-    m_sel = dot(m_all, pick)
-    m_sel = jnp.where(lax.rem(iota((n_dev * pad, prows), 0), pad) == lax.div(iota((n_dev * pad, prows), 1), blk), m_sel, 0.0)
-    mrow_s[...] = jnp.sum(m_sel.reshape(n_dev, pad, prows), axis=1)
-    same = lax.rem(iota((blk, 2 * prows), 1), blk) == iota((blk, 2 * prows), 0)
+    lane = iota((n_res, 2 * prows), 1)
+    row = iota((n_dev * pad, 2 * prows), 0)
+    col = iota((n_dev * pad, 2 * prows), 1)
+    own = jnp.logical_and(lax.rem(row, pad) == lax.div(lax.rem(col, prows), half), lax.rem(lax.div(row, pad), 2) == lax.div(col, prows))
+    for hf in range(2):
+        pick = jnp.where(iota((n_res, 2 * prows), 0) == me * blk + hf * half + lax.rem(lane, half), 1.0, 0.0).astype(BF16)
+        m_sel = jnp.where(own, dot(m_all, pick), 0.0)
+        mrow_s[hf] = jnp.sum(m_sel.reshape(chips, 2 * pad, 2 * prows), axis=1)
     qsum_s[...] = jnp.zeros_like(qsum_s)
-
-    def pair_mask(chip):
-        return jnp.concatenate([mrow_s[pl.ds(chip * 2 + core, 1), :] for core in range(2)], axis=1)
-
-    def column_in(t, carry):
-        chip = chip_at(-tile_offset(t))
-
-        def arrival(core):
+    width = 4 * prows
+    same = lax.rem(iota((half, width), 1), half) == iota((half, width), 0)
+    same_h = lax.rem(iota((heads * half, width), 1), half) == lax.rem(iota((heads * half, width), 0), half)
+
+    def lane_mask(hf, chip_a, chip_b):
+        return jnp.concatenate([mrow_s[hf, pl.ds(chip, 1), :] for chip in (chip_a, chip_b)], axis=1)
+
+    def column_in(hf, j):
+        sources = [chip_at(-tile_offset(t)) for t in (2 * j, 2 * j + 1)]
+
+        def arrival(chip, core):
             slot = slot_of(chip, core)
             pltpu.make_async_remote_copy(
-                src_ref=e1_send.at[0, 0], dst_ref=e1_recv.at[slot], send_sem=send_sem.at[0, 0], recv_sem=recv_sem.at[slot],
-                device_id={"seq": me}, device_id_type=MESH).wait_recv()
-
-        @pl.when(t == 0)
-        def _():
-            arrival(1 - c)
-
-        @pl.when(t > 0)
-        def _():
-            arrival(0)
-            arrival(1)
-
-        rows = e1_recv[pl.ds(chip * 2, 2)].reshape(2 * prows, ch)
+                src_ref=e1_send.at[0, 0, 0], dst_ref=e1_recv.at[hf, slot], send_sem=send_sem.at[0, 0, 0],
+                recv_sem=recv_sem.at[hf, slot], device_id={"seq": me}, device_id_type=MESH).wait_recv()
+
+        if j == 0:
+            arrival(sources[0], 1 - c)
+        else:
+            arrival(sources[0], 0)
+            arrival(sources[0], 1)
+        arrival(sources[1], 0)
+        arrival(sources[1], 1)
+        rows = jnp.concatenate([e1_recv[hf, pl.ds(chip * 2, 2)].reshape(2 * prows, ch) for chip in sources], axis=0)
         proj = dot(layer_norm(rows), wc_s[...]).astype(BF16)
-        kt_s[chip] = proj[:, ch:2 * ch]
-        vt_s[chip] = proj[:, 2 * ch:3 * ch]
-        gc_s[chip] = proj[:, 3 * ch:]
-        sel = jnp.where(same, pair_mask(chip), 0.0).astype(BF16)
-        qsum_s[...] += dot(sel, proj[:, :ch])
-        return carry
-
-    lax.fori_loop(0, chips, column_in, 0)
-
-    same1 = same[:, :prows]
-    count = jnp.sum(jnp.where(same1, jnp.sum(mrow_s[...], axis=0, keepdims=True), 0.0), axis=-1, keepdims=True)
-    q_mean = (qsum_s[...] / (count + MEAN_EPS)).astype(BF16)
-    q_rows = jnp.concatenate([q_mean * hm_s[h] for h in range(heads)], axis=0)
-    same_h = lax.rem(iota((hrows, 2 * prows), 1), blk) == lax.rem(iota((hrows, 2 * prows), 0), blk)
-    top = jnp.full((hrows, 2 * prows), EXCLUDED, F32)
-    for chip in range(chips):
-        x = dot_nt(q_rows, kt_s[chip]) * c2 + (MASK_BIG * LOG2E) * (pair_mask(chip) - 1.0)
-        x = jnp.where(same_h, x, EXCLUDED)
-        x_s[chip] = x
-        top = jnp.maximum(top, x)
-    top = jnp.max(top, axis=-1, keepdims=True)
-    total = jnp.zeros((hrows, 2 * prows), F32)
-    for chip in range(chips):
-        p = jnp.exp2(x_s[chip] - top)
-        total = total + p
-        for n in range(3):
-            piece = p.astype(BF16)
-            p3_s[n * hrows:(n + 1) * hrows, chip * 2 * prows:(chip + 1) * 2 * prows] = piece
-            p = p - piece.astype(F32)
-    o3 = dot(p3_s[...], vt_s[...].reshape(chips * 2 * prows, ch))
-    o = (o3[:hrows] + o3[hrows:2 * hrows] + o3[2 * hrows:]) / jnp.sum(total, axis=-1, keepdims=True)
-    co_s[...] = own_head([o[h * blk:(h + 1) * blk] for h in range(heads)])
-
+        for n, chip in enumerate(sources):
+            part = proj[n * 2 * prows:(n + 1) * 2 * prows]
+            kt_s[hf, chip] = part[:, ch:2 * ch]
+            vt_s[hf, chip] = part[:, 2 * ch:3 * ch]
+            gc_s[hf, chip] = part[:, 3 * ch:]
+        sel = jnp.where(same, lane_mask(hf, sources[0], sources[1]), 0.0).astype(BF16)
+        qsum_s[hf] += dot(sel, proj[:, :ch])
+
+    def column_attention(hf):
+        count = jnp.sum(mrow_s[hf], axis=0, keepdims=True)
+        count = jnp.sum(jnp.where(same[:, :2 * prows], count, 0.0), axis=-1, keepdims=True)
+        q_mean = (qsum_s[hf] / (count + MEAN_EPS)).astype(BF16).astype(F32)
+        q_rows = jnp.concatenate([q_mean * hm_s[h, :half].astype(F32) for h in range(heads)], axis=0).astype(BF16)
+        n_rows = heads * half
+        top = jnp.full((n_rows, width), EXCLUDED, F32)
+        for pair in range(chips // 2):
+            keys = kt_s[hf, 2 * pair:2 * pair + 2].reshape(width, ch)
+            x = dot_nt(q_rows, keys) * c2 + (MASK_BIG * LOG2E) * (lane_mask(hf, 2 * pair, 2 * pair + 1) - 1.0)
+            x = jnp.where(same_h, x, EXCLUDED)
+            x_s[pair] = x
+            top = jnp.maximum(top, x)
+        top = jnp.max(top, axis=-1, keepdims=True)
+        total = jnp.zeros((n_rows, width), F32)
+        for pair in range(chips // 2):
+            p = jnp.exp2(x_s[pair] - top)
+            total = total + p
+            for n in range(3):
+                piece = p.astype(BF16)
+                p3_s[n * n_rows:(n + 1) * n_rows, pair * width:(pair + 1) * width] = piece
+                p = p - piece.astype(F32)
+        o3 = dot(p3_s[...], vt_s[hf].reshape(chips * 2 * prows, ch))
+        o = (o3[:n_rows] + o3[n_rows:2 * n_rows] + o3[2 * n_rows:]) / jnp.sum(total, axis=-1, keepdims=True)
+        head = lane_head[:half]
+        picked = o[:half]
+        for h in range(1, heads):
+            picked = jnp.where(head == h, o[h * half:(h + 1) * half], picked)
+        co_s[...] = picked
+
+    n_out = 4 * n_seq
+
+    def out_copy(hf, pair):
+        rows = pl.ds(pair * n_out, n_out)
+        return pltpu.make_async_copy(out_v.at[hf, rows], out_hbm.at[rows, pl.ds(hf * half, half)], out_sem.at[hf, pair])
+
+    def finish_pair(hf, pair):
+        e1 = e1_recv[hf, pl.ds(pair * 4, 4)].reshape(width, ch).astype(F32)
+        gate = jax.nn.sigmoid(gc_s[hf, pl.ds(pair * 2, 2)].reshape(width, ch).astype(F32)).reshape(n_out, half, ch)
+        gated = (gate * co_s[...][None]).reshape(width, ch).astype(BF16)
+        e2 = (e1 + dot(gated, wco_v[...])).astype(BF16)
+        hidden = jnp.maximum(dot(layer_norm(e2), wti_v[...]), 0.0).astype(BF16)
+        e3 = e2.astype(F32) + dot(hidden, wto_v[...])
+        out_v[hf, pl.ds(pair * n_out, n_out)] = e3.reshape(n_out, half, ch).astype(BF16)
+        out_copy(hf, pair).start()
+
+    def finish(hf):
+        def trip(n, carry):
+            finish_pair(hf, 2 * n)
+            finish_pair(hf, 2 * n + 1)
+            return carry
+
+        lax.fori_loop(0, chips // 4, trip, 0)
+
+    relay(0)
+    second_halves(3, 5)
+    column_in(0, 0)
+    column_in(0, 1)
+    relay(1)
+    second_halves(5, chips - 1)
+    column_in(0, 2)
+    column_in(0, 3)
+    column_attention(0)
     copies[7].wait()
     copies[8].wait()
     copies[9].wait()
-
-    def finish(pair, carry):
-        for n in range(2):
-            finish_chip(pair * 2 + n)
-        return carry
-
-    def finish_chip(chip):
-        e1 = e1_recv[pl.ds(chip * 2, 2)].reshape(2 * prows, ch).astype(F32)
-        gate = jax.nn.sigmoid(gc_s[chip].astype(F32)).reshape(2 * n_seq, blk, ch)
-        gated = (gate * co_s[...][None]).astype(BF16).reshape(2 * prows, ch)
-        e2 = (e1 + dot(gated, wco_v[...])).astype(BF16)
-        hidden = jnp.maximum(dot(layer_norm(e2), wti_v[...]), 0.0).astype(BF16)
-        e3 = (e2.astype(F32) + dot(hidden, wto_v[...])).astype(BF16)
-        out_v[pl.ds(chip * 2 * n_seq, 2 * n_seq)] = e3.reshape(2 * n_seq, blk, ch)
-        out_copy(chip).start()
-
-    def out_copy(chip):
-        rows = pl.ds(chip * 2 * n_seq, 2 * n_seq)
-        return pltpu.make_async_copy(out_v.at[rows], out_hbm.at[rows], out_sem.at[chip])
-
-    lax.fori_loop(0, chips // 2, finish, 0)
+    finish(0)
+    for j in range(chips // 2):
+        column_in(1, j)
+    column_attention(1)
+    finish(1)
 
     for k in range(reach):
         up(k).wait_send()
@@ -313,12 +372,15 @@
             down(k).wait_send()
     for t in range(chips):
         across(0, t).wait_send()
-    e1_copy(0, 1 - c).wait_send()
-    for t in range(1, chips):
-        e1_copy(t, 0).wait_send()
-        e1_copy(t, 1).wait_send()
-    for chip in range(chips):
-        out_copy(chip).wait()
+    for hf in range(2):
+        e1_copy(0, 1 - c, hf).wait_send()
+        for core in range(2):
+            for t in range(1, chips - 1):
+                e1_copy(t, core, hf).wait_send()
+            hand_over(core, hf).wait_send()
+            hand_on(core, hf).wait_send()
+        for pair in range(chips // 2):
+            out_copy(hf, pair).wait()
 
 
 def solution(mesh):
@@ -329,7 +391,8 @@
         heads = w_pair_bias.shape[1]
         blk = n_res // n_dev
         chips = n_dev // 2
-        hrows, prows = heads * blk, n_seq * blk
+        half = blk // 2
+        hrows, prows = heads * blk, n_seq * half
         args = (e, m, z, w_pair_bias.T, w_row_in, w_row_out, w_col_in.T, w_col_out, w_trans_in, w_trans_out)
         scratch = [pltpu.VMEM(a.shape, a.dtype) for a in args] + [
             pltpu.VMEM((n_res // 128, hrows, 128), F32),
@@ -341,26 +404,29 @@
             pltpu.VMEM((n_seq, n_res), F32),
             pltpu.VMEM((heads, blk, ch), BF16),
             pltpu.VMEM((2 * hrows, n_res), F32),
-            pltpu.VMEM((2, n_seq, blk, ch), BF16),
-            pltpu.VMEM((chips, 2, prows, ch), BF16),
-            pltpu.VMEM((n_dev, prows, ch), BF16),
+            pltpu.VMEM((2, 2, n_seq, half, ch), F32),
+            pltpu.VMEM((chips, 2, 2, prows, ch), BF16),
+            pltpu.VMEM((2, n_dev, prows, ch), BF16),
+            pltpu.VMEM((2, 2, prows, ch), BF16),
             pltpu.VMEM((ch, 4 * ch), BF16),
-            pltpu.VMEM((n_dev, prows), F32),
-            pltpu.VMEM((blk, ch), F32),
-            pltpu.VMEM((chips, 2 * prows, ch), BF16),
-            pltpu.VMEM((chips, 2 * prows, ch), BF16),
-            pltpu.VMEM((chips, 2 * prows, ch), BF16),
-            pltpu.VMEM((chips, hrows, 2 * prows), F32),
-            pltpu.VMEM((3 * hrows, n_dev * prows), BF16),
-            pltpu.VMEM((blk, ch), F32),
-            pltpu.VMEM((n_dev * n_seq, blk, ch), BF16),
+            pltpu.VMEM((2, chips, 2 * prows), F32),
+            pltpu.VMEM((2, half, ch), F32),
+            pltpu.VMEM((2, chips, 2 * prows, ch), BF16),
+            pltpu.VMEM((2, chips, 2 * prows, ch), BF16),
+            pltpu.VMEM((2, chips, 2 * prows, ch), BF16),
+            pltpu.VMEM((chips // 2, heads * half, 4 * prows), F32),
+            pltpu.VMEM((3 * heads * half, n_dev * prows), BF16),
+            pltpu.VMEM((half, ch), F32),
+            pltpu.VMEM((2, n_dev * n_seq, half, ch), BF16),
             pltpu.SemaphoreType.DMA((len(args),)),
-            pltpu.SemaphoreType.DMA((chips,)),
+            pltpu.SemaphoreType.DMA((2, chips // 2)),
             pltpu.SemaphoreType.DMA((2, chips // 2)),
             pltpu.SemaphoreType.DMA((chips,)),
             pltpu.SemaphoreType.DMA((n_dev,)),
-            pltpu.SemaphoreType.DMA((chips, 2)),
-            pltpu.SemaphoreType.DMA((n_dev,)),
+            pltpu.SemaphoreType.DMA((chips, 2, 2)),
+            pltpu.SemaphoreType.DMA((2, n_dev)),
+            pltpu.SemaphoreType.DMA((2, 2)),
+            pltpu.SemaphoreType.DMA((2, 2)),
         ]
         return pl.pallas_call(
             functools.partial(block_kernel, (n_dev, n_seq, n_res, ch, heads)),

time: 57.1 us -> 57.6 us (level)
  no operation moved by 1% of the time
where the time goes in v4:
time: 57.6 us; the launch traced here: 57.5 us
  Pallas kernels  55.2 us (96%)
  local copies, waits for them, and re-layouts  2.26 us (4%)
    pallas_call x1, Pallas kernels, local_block(): pl.pallas_call(functools.partial(block_kernel, (n_dev, n_seq, n_res, ch,...  55.2 us
    unnamed x1, local copies, waits for them, and re-layouts  2.26 us

profile of v4, /device:TPU:21, one launch (start us, length us, event | category | flops | bytes accessed | tf_op | source)
XLA Modules:
  0.0 57.5 jit_solution(9568238445189161307)
XLA Ops:
  0.0 55.2 %msa_block.1 = bf16[128,16,256]{2,1,0:T(8,128)(2,1)} custom-call(bf16[8,256,256]{2,1,0:T(8,128)(2,1)} %e_hbm.1, s32[8,256]{1,0:T(8,128)} %m_hbm.1, bf16[16,256,128]{2,1,0:T(8,128)(2,1)} %z_hbm.1, bf16[8,128]{1,0:T(8,128)(2,1)} %bitcast.3, bf16[256,1024]{1,0:T(8,128)(2,1)} %wri_hbm.1, bf16[256,256]{1,0:T(8,128)(2,1)} %wro_hbm.1, bf16[576,256]{1,0:T(8,128)(2,1)} %bitcast.2, ...), custom_call_target="tpu_custom_call" | custom-call | tf_op jit(solution)/shard_map/msa_block/pallas_call | solution.py:431
  55.2 2.3 %copy.12 = bf16[128,16,256]{2,1,0:T(8,128)(2,1)} copy(bf16[128,16,256]{2,1,0:T(8,128)(2,1)} %msa_block.1) | data formatting | bytes 2097152

commit v5 on v4

--- a/solution.py
+++ b/solution.py
@@ -40,8 +40,8 @@
 def block_kernel(dims, e_hbm, m_hbm, z_hbm, wpb_hbm, wri_hbm, wro_hbm, wci_hbm, wco_hbm, wti_hbm, wto_hbm, out_hbm,
                  e_v, m_v, z_v, wpb_v, wri_v, wro_v, wci_v, wco_v, wti_v, wto_v,
                  bias32, bias_all, q_s, k_s, v_s, g_s, mb_s, hm_s, bias_t, gt_s, e1_send, e1_recv,
-                 relay_v, wc_s, mrow_s, qsum_s, kt_s, vt_s, gc_s, x_s, p3_s, co_s, out_v,
-                 in_sem, out_sem, chain_sem, pair_sem, bias_sem, send_sem, recv_sem, relay_sem, hand_sem):
+                 wc_s, mrow_s, qsum_s, kt_s, vt_s, gc_s, x_s, p3_s, co_s, out_v,
+                 in_sem, out_sem, chain_sem, pair_sem, bias_sem, send_sem, recv_sem):
     n_dev, n_seq, n_res, ch, heads = dims
     chips = n_dev // 2
     reach = chips // 2
@@ -138,47 +138,37 @@
             src_ref=e1_send.at[t, hf, core], dst_ref=e1_recv.at[hf, me], send_sem=send_sem.at[t, hf, core],
             recv_sem=recv_sem.at[hf, me], device_id={"seq": slot_of(tile_chip(t), core)}, device_id_type=MESH)
 
-    def hand_over(core, hf):
-        return pltpu.make_async_remote_copy(
-            src_ref=e1_send.at[chips - 1, hf, core], dst_ref=relay_v.at[core, hf], send_sem=send_sem.at[chips - 1, hf, core],
-            recv_sem=relay_sem.at[core, hf], device_id={"seq": slot_of(chip_at(1 - 2 * core), c)}, device_id_type=MESH)
-
-    def hand_on(core, hf):
-        way = 1 - 2 * core
-        source = slot_of(chip_at(-way), c)
-        return pltpu.make_async_remote_copy(
-            src_ref=relay_v.at[core, hf], dst_ref=e1_recv.at[hf, source], send_sem=hand_sem.at[core, hf],
-            recv_sem=recv_sem.at[hf, source], device_id={"seq": slot_of(chip_at(way * (reach - 1)), core)}, device_id_type=MESH)
-
-    def relay(hf):
-        for core in range(2):
-            hand_over(core, hf).wait_recv()
-            hand_on(core, hf).start()
-
     def tile_offset(t):
         k = lax.div(t + 1, 2)
-        return k * (1 - 2 * lax.rem(t, 2))
+        return k * (2 * lax.rem(t, 2) - 1)
 
     def tile_chip(t):
         return chip_at(tile_offset(t))
 
     def row_tile(t, carry):
-        k = lax.div(t + 1, 2)
-
-        @pl.when(lax.rem(t, 2) == 1)
+        k = lax.div(t, 2) + 1
+
+        @pl.when(lax.rem(t, 2) == 0)
         def _():
             bias_wait(-k, c)
-            across(-k, t).start()
 
             @pl.when(k < reach)
             def _():
                 up(k).start()
+
+            across(-k, 2 * k - 1).start()
+
+            @pl.when(k < reach)
+            def _():
                 bias_wait(k, c)
-                across(k, t + 1).start()
 
             @pl.when(k < reach - 1)
             def _():
                 down(k).start()
+
+            @pl.when(k < reach)
+            def _():
+                across(k, 2 * k).start()
 
         bias_wait(tile_offset(t), 1 - c)
         chip = tile_chip(t)
@@ -225,24 +215,25 @@
                 e1_recv[hf, me] = e1_send[0, hf, c]
                 e1_copy(0, 1 - c, hf).start()
 
-        @pl.when(jnp.logical_and(t > 0, t < chips - 1))
+        @pl.when(t > 0)
         def _():
             e1_copy(t, 0, 0).start()
             e1_copy(t, 1, 0).start()
 
+        @pl.when(jnp.logical_and(t > 0, t < 5))
+        def _():
+            e1_copy(t, 0, 1).start()
+            e1_copy(t, 1, 1).start()
+
         return carry
 
     lax.fori_loop(0, chips, row_tile, 0)
-    for hf in range(2):
-        for core in range(2):
-            hand_over(core, hf).start()
-
     def second_halves(first_t, last_t):
         for t in range(first_t, last_t):
             for core in range(2):
                 e1_copy(t, core, 1).start()
 
-    second_halves(1, 3)
+    second_halves(5, chips)
 
     copies[6].wait()
     w_k, w_v = wci_v[ch:ch + hd], wci_v[ch + hd:ch + 2 * hd]
@@ -348,12 +339,8 @@
 
         lax.fori_loop(0, chips // 4, trip, 0)
 
-    relay(0)
-    second_halves(3, 5)
     column_in(0, 0)
     column_in(0, 1)
-    relay(1)
-    second_halves(5, chips - 1)
     column_in(0, 2)
     column_in(0, 3)
     column_attention(0)
@@ -375,10 +362,8 @@
     for hf in range(2):
         e1_copy(0, 1 - c, hf).wait_send()
         for core in range(2):
-            for t in range(1, chips - 1):
+            for t in range(1, chips):
                 e1_copy(t, core, hf).wait_send()
-            hand_over(core, hf).wait_send()
-            hand_on(core, hf).wait_send()
         for pair in range(chips // 2):
             out_copy(hf, pair).wait()
 
@@ -407,7 +392,6 @@
             pltpu.VMEM((2, 2, n_seq, half, ch), F32),
             pltpu.VMEM((chips, 2, 2, prows, ch), BF16),
             pltpu.VMEM((2, n_dev, prows, ch), BF16),
-            pltpu.VMEM((2, 2, prows, ch), BF16),
             pltpu.VMEM((ch, 4 * ch), BF16),
             pltpu.VMEM((2, chips, 2 * prows), F32),
             pltpu.VMEM((2, half, ch), F32),
@@ -425,8 +409,6 @@
             pltpu.SemaphoreType.DMA((n_dev,)),
             pltpu.SemaphoreType.DMA((chips, 2, 2)),
             pltpu.SemaphoreType.DMA((2, n_dev)),
-            pltpu.SemaphoreType.DMA((2, 2)),
-            pltpu.SemaphoreType.DMA((2, 2)),
         ]
         return pl.pallas_call(
             functools.partial(block_kernel, (n_dev, n_seq, n_res, ch, heads)),

time: 57.6 us -> 56.6 us (0.983)
  Pallas kernels: 55.2 us -> 54.3 us
    pallas_call x1, Pallas kernels: 55.2 us -> 54.3 us  [local_block(): pl.pallas_call(functools.partial(block_kernel, (n_dev, n_seq, n_res, ch,...]
where the time goes in v5:
time: 56.6 us; the launch traced here: 56.5 us
  Pallas kernels  54.3 us (96%)
  local copies, waits for them, and re-layouts  2.26 us (4%)
    pallas_call x1, Pallas kernels, local_block(): pl.pallas_call(functools.partial(block_kernel, (n_dev, n_seq, n_res, ch,...  54.3 us
    unnamed x1, local copies, waits for them, and re-layouts  2.26 us

profile of v5, /device:TPU:21, one launch (start us, length us, event | category | flops | bytes accessed | tf_op | source)
XLA Modules:
  0.0 56.5 jit_solution(10228080550436656451)
XLA Ops:
  0.0 54.3 %msa_block.1 = bf16[128,16,256]{2,1,0:T(8,128)(2,1)} custom-call(bf16[8,256,256]{2,1,0:T(8,128)(2,1)} %e_hbm.1, s32[8,256]{1,0:T(8,128)} %m_hbm.1, bf16[16,256,128]{2,1,0:T(8,128)(2,1)} %z_hbm.1, bf16[8,128]{1,0:T(8,128)(2,1)} %bitcast.3, bf16[256,1024]{1,0:T(8,128)(2,1)} %wri_hbm.1, bf16[256,256]{1,0:T(8,128)(2,1)} %wro_hbm.1, bf16[576,256]{1,0:T(8,128)(2,1)} %bitcast.2, ...), custom_call_target="tpu_custom_call" | custom-call | tf_op jit(solution)/shard_map/msa_block/pallas_call | solution.py:413
  54.3 2.3 %copy.12 = bf16[128,16,256]{2,1,0:T(8,128)(2,1)} copy(bf16[128,16,256]{2,1,0:T(8,128)(2,1)} %msa_block.1) | data formatting | bytes 2097152

commit v6 on v5

--- a/solution.py
+++ b/solution.py
@@ -73,9 +73,13 @@
     copies[0].wait()
     copies[1].wait()
     wpb_t = wpb_v[...]
+    ones = jnp.ones((z_v.shape[2], z_v.shape[2]), BF16)
 
     def bias_row(i, carry):
-        rows = dot_nt(wpb_t, layer_norm(z_v[i]))
+        z_row = z_v[i]
+        centered = z_row.astype(F32) - dot(z_row, ones) * (1.0 / z_row.shape[1])
+        var = jnp.mean(centered * centered, axis=-1, keepdims=True)
+        rows = dot_nt(wpb_t, (centered * lax.rsqrt(var + LN_EPS)).astype(BF16))
         for n in range(n_res // 128):
             bias32[n, pl.ds(i, heads, stride=blk), :] = rows[:, n * 128:(n + 1) * 128]
         return carry
@@ -145,6 +149,10 @@
     def tile_chip(t):
         return chip_at(tile_offset(t))
 
+    def send(t, hf):
+        for core in range(2):
+            e1_copy(t, core, hf).start()
+
     def row_tile(t, carry):
         k = lax.div(t, 2) + 1
 
@@ -169,6 +177,16 @@
             @pl.when(k < reach)
             def _():
                 across(k, 2 * k).start()
+
+            @pl.when(t == 2)
+            def _():
+                send(1, 0)
+
+            @pl.when(t == 4)
+            def _():
+                send(3, 0)
+                send(1, 1)
+                send(2, 1)
 
         bias_wait(tile_offset(t), 1 - c)
         chip = tile_chip(t)
@@ -215,25 +233,15 @@
                 e1_recv[hf, me] = e1_send[0, hf, c]
                 e1_copy(0, 1 - c, hf).start()
 
-        @pl.when(t > 0)
+        @pl.when(jnp.logical_or(t == 2, t > 3))
         def _():
-            e1_copy(t, 0, 0).start()
-            e1_copy(t, 1, 0).start()
-
-        @pl.when(jnp.logical_and(t > 0, t < 5))
-        def _():
-            e1_copy(t, 0, 1).start()
-            e1_copy(t, 1, 1).start()
+            send(t, 0)
 
         return carry
 
     lax.fori_loop(0, chips, row_tile, 0)
-    def second_halves(first_t, last_t):
-        for t in range(first_t, last_t):
-            for core in range(2):
-                e1_copy(t, core, 1).start()
-
-    second_halves(5, chips)
+    for t in range(3, chips):
+        send(t, 1)
 
     copies[6].wait()
     w_k, w_v = wci_v[ch:ch + hd], wci_v[ch + hd:ch + 2 * hd]

time: 56.6 us -> 54.5 us (0.963)
  Pallas kernels: 54.3 us -> 52.1 us
    pallas_call x1, Pallas kernels: 54.3 us -> 52.1 us  [local_block(): pl.pallas_call(functools.partial(block_kernel, (n_dev, n_seq, n_res, ch,...]
where the time goes in v6:
time: 54.5 us; the launch traced here: 54.4 us
  Pallas kernels  52.1 us (96%)
  local copies, waits for them, and re-layouts  2.26 us (4%)
    pallas_call x1, Pallas kernels, local_block(): pl.pallas_call(functools.partial(block_kernel, (n_dev, n_seq, n_res, ch,...  52.1 us
    unnamed x1, local copies, waits for them, and re-layouts  2.26 us

profile of v6, /device:TPU:21, one launch (start us, length us, event | category | flops | bytes accessed | tf_op | source)
XLA Modules:
  0.0 54.4 jit_solution(416544193696379766)
XLA Ops:
  0.0 52.1 %msa_block.1 = bf16[128,16,256]{2,1,0:T(8,128)(2,1)} custom-call(bf16[8,256,256]{2,1,0:T(8,128)(2,1)} %e_hbm.1, s32[8,256]{1,0:T(8,128)} %m_hbm.1, bf16[16,256,128]{2,1,0:T(8,128)(2,1)} %z_hbm.1, bf16[8,128]{1,0:T(8,128)(2,1)} %bitcast.3, bf16[256,1024]{1,0:T(8,128)(2,1)} %wri_hbm.1, bf16[256,256]{1,0:T(8,128)(2,1)} %wro_hbm.1, bf16[576,256]{1,0:T(8,128)(2,1)} %bitcast.2, ...), custom_call_target="tpu_custom_call" | custom-call | tf_op jit(solution)/shard_map/msa_block/pallas_call | solution.py:421
  52.1 2.3 %copy.12 = bf16[128,16,256]{2,1,0:T(8,128)(2,1)} copy(bf16[128,16,256]{2,1,0:T(8,128)(2,1)} %msa_block.1) | data formatting | bytes 2097152

commit v7 on v6

--- a/solution.py
+++ b/solution.py
@@ -37,11 +37,11 @@
     return lax.broadcasted_iota(jnp.int32, shape, dim)
 
 
-def block_kernel(dims, e_hbm, m_hbm, z_hbm, wpb_hbm, wri_hbm, wro_hbm, wci_hbm, wco_hbm, wti_hbm, wto_hbm, out_hbm,
+def block_kernel(dims, e_hbm, m_hbm, z_hbm, wpb_hbm, wri_hbm, wro_hbm, wci_hbm, wco_hbm, wti_hbm, wto_hbm, out_ref,
                  e_v, m_v, z_v, wpb_v, wri_v, wro_v, wci_v, wco_v, wti_v, wto_v,
                  bias32, bias_all, q_s, k_s, v_s, g_s, mb_s, hm_s, bias_t, gt_s, e1_send, e1_recv,
-                 wc_s, mrow_s, qsum_s, kt_s, vt_s, gc_s, x_s, p3_s, co_s, out_v,
-                 in_sem, out_sem, chain_sem, pair_sem, bias_sem, send_sem, recv_sem):
+                 wc_s, mrow_s, qsum_s, kt_s, vt_s, gc_s, x_s, p3_s, co_s,
+                 in_sem, chain_sem, pair_sem, bias_sem, send_sem, recv_sem):
     n_dev, n_seq, n_res, ch, heads = dims
     chips = n_dev // 2
     reach = chips // 2
@@ -92,26 +92,29 @@
     bias_all[me, hrows:] = jnp.concatenate([m_f32, m_f32], axis=0).astype(BF16)
     pl.semaphore_wait(barrier, n_dev - 1)
 
-    def bias_copy(slot, sem, chip, core):
+    def bias_copy(slot, sem, chip, core, part):
+        rows = pl.ds(0, hrows // 2) if part == 0 else pl.ds(hrows // 2, hrows // 2 + 2 * n_seq)
         return pltpu.make_async_remote_copy(
-            src_ref=bias_all.at[slot], dst_ref=bias_all.at[slot], send_sem=sem, recv_sem=bias_sem.at[slot],
-            device_id={"seq": slot_of(chip, core)}, device_id_type=MESH)
-
-    def up(k):
-        return bias_copy(slot_of(chip_at(-k), c), chain_sem.at[0, k], chip_at(1), c)
-
-    def down(k):
-        return bias_copy(slot_of(chip_at(k), c), chain_sem.at[1, k], chip_at(-1), c)
-
-    def across(offset, t):
-        return bias_copy(slot_of(chip_at(offset), c), pair_sem.at[t], z, 1 - c)
-
-    def bias_wait(offset, core):
-        bias_copy(slot_of(chip_at(offset), core), pair_sem.at[0], z, c).wait_recv()
-
-    up(0).start()
-    down(0).start()
-    across(0, 0).start()
+            src_ref=bias_all.at[slot, rows], dst_ref=bias_all.at[slot, rows], send_sem=sem.at[part],
+            recv_sem=bias_sem.at[slot, part], device_id={"seq": slot_of(chip, core)}, device_id_type=MESH)
+
+    def up(k, part):
+        return bias_copy(slot_of(chip_at(-k), c), chain_sem.at[0, k], chip_at(1), c, part)
+
+    def down(k, part):
+        return bias_copy(slot_of(chip_at(k), c), chain_sem.at[1, k], chip_at(-1), c, part)
+
+    def across(offset, t, part):
+        return bias_copy(slot_of(chip_at(offset), c), pair_sem.at[t], z, 1 - c, part)
+
+    def bias_wait(offset, core, part):
+        bias_copy(slot_of(chip_at(offset), core), pair_sem.at[0], z, c, part).wait_recv()
+
+    for part in range(2):
+        up(0, part).start()
+        down(0, part).start()
+    for part in range(2):
+        across(0, 0, part).start()
 
     for h in range(heads):
         hm_s[h] = jnp.where(lax.div(iota((blk, ch), 1), hd) == h, 1.0, 0.0).astype(BF16)
@@ -158,25 +161,26 @@
 
         @pl.when(lax.rem(t, 2) == 0)
         def _():
-            bias_wait(-k, c)
-
-            @pl.when(k < reach)
-            def _():
-                up(k).start()
-
-            across(-k, 2 * k - 1).start()
-
-            @pl.when(k < reach)
-            def _():
-                bias_wait(k, c)
-
-            @pl.when(k < reach - 1)
-            def _():
-                down(k).start()
-
-            @pl.when(k < reach)
-            def _():
-                across(k, 2 * k).start()
+            for part in range(2):
+                bias_wait(-k, c, part)
+
+                @pl.when(k < reach)
+                def _():
+                    up(k, part).start()
+
+                across(-k, 2 * k - 1, part).start()
+
+                @pl.when(k < reach)
+                def _():
+                    bias_wait(k, c, part)
+
+                @pl.when(k < reach - 1)
+                def _():
+                    down(k, part).start()
+
+                @pl.when(k < reach)
+                def _():
+                    across(k, 2 * k, part).start()
 
             @pl.when(t == 2)
             def _():
@@ -188,7 +192,8 @@
                 send(1, 1)
                 send(2, 1)
 
-        bias_wait(tile_offset(t), 1 - c)
+        bias_wait(tile_offset(t), 1 - c, 0)
+        bias_wait(tile_offset(t), 1 - c, 1)
         chip = tile_chip(t)
         for core in range(2):
             bias_t[core * hrows:(core + 1) * hrows] = bias_all[slot_of(chip, core), :hrows].astype(F32) * LOG2E
@@ -325,10 +330,6 @@
 
     n_out = 4 * n_seq
 
-    def out_copy(hf, pair):
-        rows = pl.ds(pair * n_out, n_out)
-        return pltpu.make_async_copy(out_v.at[hf, rows], out_hbm.at[rows, pl.ds(hf * half, half)], out_sem.at[hf, pair])
-
     def finish_pair(hf, pair):
         e1 = e1_recv[hf, pl.ds(pair * 4, 4)].reshape(width, ch).astype(F32)
         gate = jax.nn.sigmoid(gc_s[hf, pl.ds(pair * 2, 2)].reshape(width, ch).astype(F32)).reshape(n_out, half, ch)
@@ -336,16 +337,11 @@
         e2 = (e1 + dot(gated, wco_v[...])).astype(BF16)
         hidden = jnp.maximum(dot(layer_norm(e2), wti_v[...]), 0.0).astype(BF16)
         e3 = e2.astype(F32) + dot(hidden, wto_v[...])
-        out_v[hf, pl.ds(pair * n_out, n_out)] = e3.reshape(n_out, half, ch).astype(BF16)
-        out_copy(hf, pair).start()
+        out_ref[pair * n_out:(pair + 1) * n_out, hf * half:(hf + 1) * half, :] = e3.reshape(n_out, half, ch).astype(BF16)
 
     def finish(hf):
-        def trip(n, carry):
-            finish_pair(hf, 2 * n)
-            finish_pair(hf, 2 * n + 1)
-            return carry
-
-        lax.fori_loop(0, chips // 4, trip, 0)
+        for pair in range(chips // 2):
+            finish_pair(hf, pair)
 
     column_in(0, 0)
     column_in(0, 1)
@@ -361,19 +357,18 @@
     column_attention(1)
     finish(1)
 
-    for k in range(reach):
-        up(k).wait_send()
-        if k < reach - 1:
-            down(k).wait_send()
-    for t in range(chips):
-        across(0, t).wait_send()
+    for part in range(2):
+        for k in range(reach):
+            up(k, part).wait_send()
+            if k < reach - 1:
+                down(k, part).wait_send()
+        for t in range(chips):
+            across(0, t, part).wait_send()
     for hf in range(2):
         e1_copy(0, 1 - c, hf).wait_send()
         for core in range(2):
             for t in range(1, chips):
                 e1_copy(t, core, hf).wait_send()
-        for pair in range(chips // 2):
-            out_copy(hf, pair).wait()
 
 
 def solution(mesh):
@@ -409,20 +404,18 @@
             pltpu.VMEM((chips // 2, heads * half, 4 * prows), F32),
             pltpu.VMEM((3 * heads * half, n_dev * prows), BF16),
             pltpu.VMEM((half, ch), F32),
-            pltpu.VMEM((2, n_dev * n_seq, half, ch), BF16),
             pltpu.SemaphoreType.DMA((len(args),)),
-            pltpu.SemaphoreType.DMA((2, chips // 2)),
-            pltpu.SemaphoreType.DMA((2, chips // 2)),
-            pltpu.SemaphoreType.DMA((chips,)),
-            pltpu.SemaphoreType.DMA((n_dev,)),
+            pltpu.SemaphoreType.DMA((2, chips // 2, 2)),
+            pltpu.SemaphoreType.DMA((chips, 2)),
+            pltpu.SemaphoreType.DMA((n_dev, 2)),
             pltpu.SemaphoreType.DMA((chips, 2, 2)),
             pltpu.SemaphoreType.DMA((2, n_dev)),
         ]
         return pl.pallas_call(
             functools.partial(block_kernel, (n_dev, n_seq, n_res, ch, heads)),
-            out_shape=jax.ShapeDtypeStruct((n_dev * n_seq, blk, ch), BF16),
+            out_shape=pltpu.VMEM((n_dev * n_seq, blk, ch), BF16),
             in_specs=[pl.BlockSpec(memory_space=pl.ANY)] * len(args),
-            out_specs=pl.BlockSpec(memory_space=pl.ANY),
+            out_specs=pl.BlockSpec(memory_space=pltpu.VMEM),
             scratch_shapes=scratch,
             name="msa_block",
             compiler_params=pltpu.CompilerParams(collective_id=0, has_side_effects=True, vmem_limit_bytes=60 * 2 ** 20),

time: 54.5 us -> 51.8 us (0.950)
  Pallas kernels: 52.1 us -> 50.8 us
  local copies, waits for them, and re-layouts: 2.26 us -> 0.97 us
    pallas_call x1, Pallas kernels: 52.1 us -> 50.8 us  [local_block(): pl.pallas_call(functools.partial(block_kernel, (n_dev, n_seq, n_res, ch,...]
    unnamed x1, local copies, waits for them, and re-layouts: 2.26 us -> 0.97 us
where the time goes in v7:
time: 51.8 us
  Pallas kernels  50.8 us (98%)
  local copies, waits for them, and re-layouts  0.97 us (2%)
    pallas_call x1, Pallas kernels, local_block(): pl.pallas_call(functools.partial(block_kernel, (n_dev, n_seq, n_res, ch,...  50.8 us

profile of v7, /device:TPU:21, one launch (start us, length us, event | category | flops | bytes accessed | tf_op | source)
XLA Modules:
  0.0 51.8 jit_solution(2688320038334544412)
XLA Ops:
  0.0 50.8 %msa_block.1 = bf16[128,16,256]{2,1,0:T(8,128)(2,1)S(1)} custom-call(bf16[8,256,256]{2,1,0:T(8,128)(2,1)} %e_hbm.1, s32[8,256]{1,0:T(8,128)} %m_hbm.1, bf16[16,256,128]{2,1,0:T(8,128)(2,1)} %z_hbm.1, bf16[8,128]{1,0:T(8,128)(2,1)} %bitcast.3, bf16[256,1024]{1,0:T(8,128)(2,1)} %wri_hbm.1, bf16[256,256]{1,0:T(8,128)(2,1)} %wro_hbm.1, ...), custom_call_target="tpu_custom_call" | custom-call | tf_op jit(solution)/shard_map/msa_block/pallas_call | solution.py:414
  50.8 1.0 %copy.12 = bf16[128,16,256]{2,1,0:T(8,128)(2,1)} copy(bf16[128,16,256]{2,1,0:T(8,128)(2,1)S(1)} %msa_block.1) | data formatting | bytes 2097152

commit v8 on v7

--- a/solution.py
+++ b/solution.py
@@ -185,12 +185,11 @@
             @pl.when(t == 2)
             def _():
                 send(1, 0)
+                send(1, 1)
 
             @pl.when(t == 4)
             def _():
                 send(3, 0)
-                send(1, 1)
-                send(2, 1)
 
         bias_wait(tile_offset(t), 1 - c, 0)
         bias_wait(tile_offset(t), 1 - c, 1)
@@ -241,6 +240,10 @@
         @pl.when(jnp.logical_or(t == 2, t > 3))
         def _():
             send(t, 0)
+
+        @pl.when(t == 2)
+        def _():
+            send(2, 1)
 
         return carry
 

time: 51.8 us -> 51.7 us (level)
  no operation moved by 1% of the time
where the time goes in v8:
time: 51.7 us; the launch traced here: 51.6 us
  Pallas kernels  50.6 us (98%)
  local copies, waits for them, and re-layouts  0.97 us (2%)
    pallas_call x1, Pallas kernels, local_block(): pl.pallas_call(functools.partial(block_kernel, (n_dev, n_seq, n_res, ch,...  50.6 us

profile of v8, /device:TPU:21, one launch (start us, length us, event | category | flops | bytes accessed | tf_op | source)
XLA Modules:
  0.0 51.6 jit_solution(8423643926349211493)
XLA Ops:
  0.0 50.6 %msa_block.1 = bf16[128,16,256]{2,1,0:T(8,128)(2,1)S(1)} custom-call(bf16[8,256,256]{2,1,0:T(8,128)(2,1)} %e_hbm.1, s32[8,256]{1,0:T(8,128)} %m_hbm.1, bf16[16,256,128]{2,1,0:T(8,128)(2,1)} %z_hbm.1, bf16[8,128]{1,0:T(8,128)(2,1)} %bitcast.3, bf16[256,1024]{1,0:T(8,128)(2,1)} %wri_hbm.1, bf16[256,256]{1,0:T(8,128)(2,1)} %wro_hbm.1, ...), custom_call_target="tpu_custom_call" | custom-call | tf_op jit(solution)/shard_map/msa_block/pallas_call | solution.py:417
  50.6 1.0 %copy.12 = bf16[128,16,256]{2,1,0:T(8,128)(2,1)} copy(bf16[128,16,256]{2,1,0:T(8,128)(2,1)S(1)} %msa_block.1) | data formatting | bytes 2097152

commit v9 on v8

--- a/solution.py
+++ b/solution.py
@@ -63,8 +63,8 @@
     loads = [(z_hbm, z_v), (wpb_hbm, wpb_v), (e_hbm, e_v), (m_hbm, m_v), (wri_hbm, wri_v), (wro_hbm, wro_v),
              (wci_hbm, wci_v), (wco_hbm, wco_v), (wti_hbm, wti_v), (wto_hbm, wto_v)]
     copies = [pltpu.make_async_copy(src, dst, in_sem.at[n]) for n, (src, dst) in enumerate(loads)]
-    for copy in copies:
-        copy.start()
+    copies[0].start()
+    copies[1].start()
 
     barrier = pltpu.get_barrier_semaphore()
     for d in range(1, n_dev):
@@ -72,6 +72,8 @@
 
     copies[0].wait()
     copies[1].wait()
+    for copy in copies[2:]:
+        copy.start()
     wpb_t = wpb_v[...]
     ones = jnp.ones((z_v.shape[2], z_v.shape[2]), BF16)
 
@@ -248,7 +250,7 @@
         return carry
 
     lax.fori_loop(0, chips, row_tile, 0)
-    for t in range(3, chips):
+    for t in [chips - 1] + list(range(chips - 3, chips - 1)) + list(range(3, chips - 3)):
         send(t, 1)
 
     copies[6].wait()
@@ -355,7 +357,7 @@
     copies[8].wait()
     copies[9].wait()
     finish(0)
-    for j in range(chips // 2):
+    for j in [0] + list(range(chips // 2 - 1, 0, -1)):
         column_in(1, j)
     column_attention(1)
     finish(1)

time: 51.7 us -> 51.8 us (level)
  no operation moved by 1% of the time
where the time goes in v9:
time: 51.8 us; the launch traced here: 51.7 us
  Pallas kernels  50.7 us (98%)
  local copies, waits for them, and re-layouts  0.97 us (2%)
    pallas_call x1, Pallas kernels, local_block(): pl.pallas_call(functools.partial(block_kernel, (n_dev, n_seq, n_res, ch,...  50.7 us

profile of v9, /device:TPU:21, one launch (start us, length us, event | category | flops | bytes accessed | tf_op | source)
XLA Modules:
  0.0 51.7 jit_solution(6306610635566410990)
XLA Ops:
  0.0 50.7 %msa_block.1 = bf16[128,16,256]{2,1,0:T(8,128)(2,1)S(1)} custom-call(bf16[8,256,256]{2,1,0:T(8,128)(2,1)} %e_hbm.1, s32[8,256]{1,0:T(8,128)} %m_hbm.1, bf16[16,256,128]{2,1,0:T(8,128)(2,1)} %z_hbm.1, bf16[8,128]{1,0:T(8,128)(2,1)} %bitcast.3, bf16[256,1024]{1,0:T(8,128)(2,1)} %wri_hbm.1, bf16[256,256]{1,0:T(8,128)(2,1)} %wro_hbm.1, ...), custom_call_target="tpu_custom_call" | custom-call | tf_op jit(solution)/shard_map/msa_block/pallas_call | solution.py:419
  50.7 1.0 %copy.12 = bf16[128,16,256]{2,1,0:T(8,128)(2,1)} copy(bf16[128,16,256]{2,1,0:T(8,128)(2,1)S(1)} %msa_block.1) | data formatting | bytes 2097152

commit v10 on v9

--- a/solution.py
+++ b/solution.py
@@ -250,7 +250,7 @@
         return carry
 
     lax.fori_loop(0, chips, row_tile, 0)
-    for t in [chips - 1] + list(range(chips - 3, chips - 1)) + list(range(3, chips - 3)):
+    for t in range(3, chips):
         send(t, 1)
 
     copies[6].wait()
@@ -357,7 +357,7 @@
     copies[8].wait()
     copies[9].wait()
     finish(0)
-    for j in [0] + list(range(chips // 2 - 1, 0, -1)):
+    for j in range(chips // 2):
         column_in(1, j)
     column_attention(1)
     finish(1)

time: 51.8 us -> 51.3 us (level)
  no operation moved by 1% of the time
where the time goes in v10:
time: 51.3 us; the launch traced here: 51.2 us
  Pallas kernels  50.2 us (98%)
  local copies, waits for them, and re-layouts  0.97 us (2%)
    pallas_call x1, Pallas kernels, local_block(): pl.pallas_call(functools.partial(block_kernel, (n_dev, n_seq, n_res, ch,...  50.2 us

profile of v10, /device:TPU:21, one launch (start us, length us, event | category | flops | bytes accessed | tf_op | source)
XLA Modules:
  0.0 51.2 jit_solution(504664044192177995)
XLA Ops:
  0.0 50.2 %msa_block.1 = bf16[128,16,256]{2,1,0:T(8,128)(2,1)S(1)} custom-call(bf16[8,256,256]{2,1,0:T(8,128)(2,1)} %e_hbm.1, s32[8,256]{1,0:T(8,128)} %m_hbm.1, bf16[16,256,128]{2,1,0:T(8,128)(2,1)} %z_hbm.1, bf16[8,128]{1,0:T(8,128)(2,1)} %bitcast.3, bf16[256,1024]{1,0:T(8,128)(2,1)} %wri_hbm.1, bf16[256,256]{1,0:T(8,128)(2,1)} %wro_hbm.1, ...), custom_call_target="tpu_custom_call" | custom-call | tf_op jit(solution)/shard_map/msa_block/pallas_call | solution.py:419
  50.2 1.0 %copy.12 = bf16[128,16,256]{2,1,0:T(8,128)(2,1)} copy(bf16[128,16,256]{2,1,0:T(8,128)(2,1)S(1)} %msa_block.1) | data formatting | bytes 2097152
